TPU v7x, 32 devices: a whole 2x2x4 slice. The times are simulated.
32 devices in a mesh: row: 2 (over x), col: 16 (over z, y, core).
Axes of the slice: x: 2, y: 2, z: 4, core: 2. Of those that a mesh axis runs over, the one named last changes fastest.
Arguments:
- tokens: bfloat16 [64, 128, 1024], P('row', 'col'), may hold values from -6 to 6
- shifts: int32 [2], replicated, may hold values from 0 to 15
- qkv_weight: bfloat16 [1024, 3, 1024], P('col', None, 'row'), may hold values from -0.1875 to 0.1875
- out_weight: bfloat16 [1024, 1024], P('row', 'col'), may hold values from -0.1875 to 0.1875
- up_weight: bfloat16 [1024, 4096], P('col', 'row'), may hold values from -0.1875 to 0.1875
- down_weight: bfloat16 [4096, 1024], P('row', 'col'), may hold values from -0.09375 to 0.09375
- qk_gain: float32 [1024], P('row'), may hold values from 0.5 to 1.5
- attn_rate: float32 [1024], replicated, may hold values from 0.1 to 0.6
- mlp_rate: float32 [1024], replicated, may hold values from 0.1 to 0.6
- hidden_gain: float32 [4096], P('row'), may hold values from 0.5 to 2
Outputs:
- sphere_out: bfloat16 [64, 128, 1024], P('row', 'col')
Inputs may be any that keep to these rules, and one draw needn't show every extreme that they name: shifts[0] offsets the windows along rows, shifts[1] along columns.
All inputs are finite; a program needn't handle non-finite values.
Results may differ from a plain program's by a relative error of at most 0.012.
Values may be sent and summed in bfloat16 or wider, within the bound.
A program may use at most 128 MiB of HBM per device.

v0:
```python
import functools
import math

import jax
import jax.numpy as jnp
from jax import lax
from jax.experimental import pallas as pl
from jax.experimental.pallas import tpu as pltpu
from jax.sharding import PartitionSpec as P

HD = 64
WIN = 16
MESH = pl.DeviceIdType.MESH
VMEM = pl.BlockSpec(memory_space=pltpu.VMEM)


def shifted(value, axis, steps):
    count = lax.axis_size(axis)
    pairs = [(source, (source + steps) % count) for source in range(count)]
    return lax.ppermute(value, axis, pairs)


def to_sphere(vector):
    return vector * lax.rsqrt(jnp.mean(vector * vector, axis=-1, keepdims=True) + 1e-06)


class Ring:
    def __init__(self, n_row, n_col, send_sem, recv_sem):
        self.n_row, self.n_col, self.nz = n_row, n_col, n_col // 4
        self.send_sem, self.recv_sem = send_sem, recv_sem
        self.row, self.col = lax.axis_index("row"), lax.axis_index("col")
        self.z, self.y, self.core = self.col // 4, (self.col // 2) % 2, self.col % 2
        self.z_next = (self.row, self.at(self.z + 1, self.y, self.core))
        self.z_prev = (self.row, self.at(self.z - 1, self.y, self.core))
        self.y_peer = (self.row, self.at(self.z, 1 - self.y, self.core))
        self.core_peer = (self.row, self.at(self.z, self.y, 1 - self.core))
        self.started, self.core_copies, self.z_copy, self.y_copy = [], [], {}, {}

    def at(self, z, y, core):
        return (lax.rem(z + 2 * self.nz, self.nz) * 2 + y) * 2 + core

    def other_row(self, r):
        return (lax.rem(self.row + r, self.n_row), self.col)

    def greet(self, more):
        peers = [self.z_next, self.z_prev, self.y_peer, self.core_peer] + more
        peers += [self.other_row(r) for r in range(1, self.n_row)]
        barrier = pltpu.get_barrier_semaphore()
        for peer in peers:
            pl.semaphore_signal(barrier, inc=1, device_id=peer, device_id_type=MESH)
        pl.semaphore_wait(barrier, len(peers))

    def send(self, src, dst, peer):
        index = len(self.started)
        copy = pltpu.make_async_remote_copy(
            src_ref=src,
            dst_ref=dst,
            send_sem=self.send_sem.at[index],
            recv_sem=self.recv_sem.at[index],
            device_id=peer,
            device_id_type=MESH,
        )
        copy.start()
        self.started.append(copy)
        return copy

    def begin(self, w_in, w_out):
        for w in range(len(w_in)):
            slot = w_out[w].at[self.col]
            self.z_copy[w, 0] = self.send(w_in[w], slot, self.z_next)
            self.y_copy[w, 0] = self.send(w_in[w], slot, self.y_peer)
            self.core_copies.append(self.send(w_in[w], slot, self.core_peer))
        for w in range(len(w_in)):
            w_out[w][self.col] = w_in[w][...]

    def advance(self, t, w_out):
        for w in range(len(w_out)):
            if t > 0:
                self.z_copy[w, t - 1].wait_recv()
                block = w_out[w].at[self.at(self.z - t, self.y, self.core)]
                if t < self.nz - 1:
                    self.z_copy[w, t] = self.send(block, block, self.z_next)
                self.y_copy[w, t] = self.send(block, block, self.y_peer)
                self.core_copies.append(self.send(block, block, self.core_peer))
        last = t == self.nz - 1
        for late in ([t - 1] if t > 0 else []) + ([t] if last else []):
            for w in range(len(w_out)):
                self.y_copy[w, late].wait_recv()
                other = w_out[w].at[self.at(self.z - late, 1 - self.y, self.core)]
                self.core_copies.append(self.send(other, other, self.core_peer))

    def finish(self):
        for copy in self.core_copies:
            copy.wait_recv()
        for copy in self.started:
            copy.wait_send()


def gather_kernel(n_row, n_col, reach, n_weights, *refs):
    tok_in = refs[0]
    w_in = refs[1 : 1 + n_weights]
    tok_out = refs[1 + n_weights]
    w_out = refs[2 + n_weights : 2 + 2 * n_weights]
    ring = Ring(n_row, n_col, *refs[2 + 2 * n_weights :])
    row, col = ring.row, ring.col
    ring.greet(
        [(row, lax.rem(col + k, n_col)) for k in range(1, reach + 1)]
        + [(row, lax.rem(col - k + n_col, n_col)) for k in range(1, reach + 1)]
    )
    near = {}
    far = []
    for k in range(1, reach + 1):
        near[k] = ring.send(tok_in, tok_out.at[row, k], (row, lax.rem(col - k + n_col, n_col)))
    for r in range(1, n_row):
        far.append(ring.send(tok_in, tok_out.at[row, 0], ring.other_row(r)))
    ring.begin(w_in, w_out)
    tok_out[row, 0] = tok_in[...]
    for t in range(ring.nz):
        if t == 1:
            for k in range(1, reach + 1):
                near[k].wait_recv()
                piece = tok_out.at[row, k]
                for r in range(1, n_row):
                    far.append(ring.send(piece, piece, ring.other_row(r)))
        ring.advance(t, w_out)
    for copy in far:
        copy.wait_recv()
    ring.finish()


def ring_copies(n_col, n_weights):
    nz = n_col // 4
    return n_weights * (nz - 1 + nz + 2 * nz)


def gather_all(tokens, weights, n_row, n_col, reach):
    n_weights = len(weights)
    copies = reach * n_row + (n_row - 1) + ring_copies(n_col, n_weights)
    return pl.pallas_call(
        functools.partial(gather_kernel, n_row, n_col, reach, n_weights),
        out_shape=[jax.ShapeDtypeStruct((n_row, reach + 1) + tokens.shape, tokens.dtype)]
        + [jax.ShapeDtypeStruct((n_col,) + w.shape, w.dtype) for w in weights],
        in_specs=[VMEM] * (1 + n_weights),
        out_specs=[VMEM] * (1 + n_weights),
        scratch_shapes=[pltpu.SemaphoreType.DMA((copies,)), pltpu.SemaphoreType.DMA((copies,))],
        compiler_params=pltpu.CompilerParams(
            collective_id=0, has_side_effects=True, vmem_limit_bytes=48 * 1024 * 1024
        ),
        name="gather_all",
    )(tokens, *weights)


def attention_kernel(n_row, n_col, per_window, heads, band, n_weights, *refs):
    x_ref, qkv_ref, out_w_ref, gain_ref = refs[:4]
    w_in = refs[4 : 4 + n_weights]
    terms = refs[4 + n_weights]
    w_out = refs[5 + n_weights : 5 + 2 * n_weights]
    q_all, kv_all, sem_a, sem_b, kv_send, kv_recv, row_send, row_recv = refs[5 + 2 * n_weights :]
    ring = Ring(n_row, n_col, sem_a, sem_b)
    row, col = ring.row, ring.col
    bands = x_ref.shape[0] // band
    width = heads * HD
    contract = (((1,), (1,)), ((), ()))
    seat = lax.rem(col, per_window)

    def mate(k):
        return (row, col - seat + lax.rem(seat + k, per_window))

    ring.greet([mate(k) for k in range(1, per_window)])
    ring.begin(w_in, w_out)

    def band_rows(b):
        return pl.ds(pl.multiple_of(b * band, band), band)

    def kv_copy(b, k):
        return pltpu.make_async_remote_copy(
            src_ref=kv_all.at[0, :, band_rows(b)],
            dst_ref=kv_all.at[k, :, band_rows(b)],
            send_sem=kv_send.at[b, k],
            recv_sem=kv_recv.at[b, k],
            device_id=mate(k),
            device_id_type=MESH,
        )

    def row_copy(b, r):
        return pltpu.make_async_remote_copy(
            src_ref=terms.at[0, band_rows(b)],
            dst_ref=terms.at[r, band_rows(b)],
            send_sem=row_send.at[b, r],
            recv_sem=row_recv.at[b, r],
            device_id=ring.other_row(r),
            device_id_type=MESH,
        )

    def project(b, carry):
        here = band_rows(b)
        projected = jnp.dot(x_ref[here, :], qkv_ref[...], preferred_element_type=jnp.float32)
        for part in range(2):
            for head in range(heads):
                lo = head * HD
                piece = projected[:, part * width + lo : part * width + lo + HD]
                scaled = (to_sphere(piece) * gain_ref[:, lo : lo + HD]).astype(jnp.bfloat16)
                if part == 0:
                    q_all[here, lo : lo + HD] = scaled
                else:
                    kv_all[0, 0, here, lo : lo + HD] = scaled
        kv_all[0, 1, here, :] = projected[:, 2 * width :].astype(jnp.bfloat16)
        for k in range(1, per_window):
            kv_copy(b, k).start()
        return carry

    lax.fori_loop(0, bands, project, 0)
    for t in range(ring.nz // 2):
        ring.advance(t, w_out)

    def attend(b, carry):
        here = band_rows(b)
        for k in range(1, per_window):
            kv_copy(b, k).wait_recv()
        outs = []
        for head in range(heads):
            cut = slice(head * HD, head * HD + HD)
            query = q_all[here, cut]
            keys = jnp.concatenate([kv_all[k, 0, here, cut] for k in range(per_window)], axis=0)
            values = jnp.concatenate([kv_all[k, 1, here, cut] for k in range(per_window)], axis=0)
            scores = lax.dot_general(query, keys, contract, preferred_element_type=jnp.float32)
            expo = jnp.exp(scores * (1.0 / math.sqrt(HD)))
            weights = (expo / jnp.sum(expo, axis=-1, keepdims=True)).astype(jnp.bfloat16)
            outs.append(
                jnp.dot(weights, values, preferred_element_type=jnp.float32).astype(jnp.bfloat16)
            )
        attended = jnp.concatenate(outs, axis=1)
        terms[0, here, :] = lax.dot_general(
            attended, out_w_ref[...], contract, preferred_element_type=jnp.float32
        ).astype(jnp.bfloat16)
        for r in range(1, n_row):
            row_copy(b, r).start()
        return carry

    lax.fori_loop(0, bands, attend, 0)
    for t in range(ring.nz // 2, ring.nz):
        ring.advance(t, w_out)
    ring.finish()

    def drain(b, carry):
        for k in range(1, per_window):
            kv_copy(b, k).wait_send()
        for r in range(1, n_row):
            row_copy(b, r).wait()
        return carry

    lax.fori_loop(0, bands, drain, 0)


def attention(x, qkv, out_w, gain, weights, n_row, n_col, per_window, band):
    tokens, depth = x.shape
    width = qkv.shape[1] // 3
    heads = width // HD
    bands = tokens // band
    n_weights = len(weights)
    copies = ring_copies(n_col, n_weights)
    dma = pltpu.SemaphoreType.DMA
    return pl.pallas_call(
        functools.partial(attention_kernel, n_row, n_col, per_window, heads, band, n_weights),
        out_shape=[jax.ShapeDtypeStruct((n_row, tokens, depth), jnp.bfloat16)]
        + [jax.ShapeDtypeStruct((n_col,) + w.shape, w.dtype) for w in weights],
        in_specs=[VMEM] * (4 + n_weights),
        out_specs=[VMEM] * (1 + n_weights),
        scratch_shapes=[
            pltpu.VMEM((tokens, width), jnp.bfloat16),
            pltpu.VMEM((per_window, 2, tokens, width), jnp.bfloat16),
            dma((copies,)),
            dma((copies,)),
            dma((bands, per_window)),
            dma((bands, per_window)),
            dma((bands, n_row)),
            dma((bands, n_row)),
        ],
        compiler_params=pltpu.CompilerParams(
            collective_id=1, has_side_effects=True, vmem_limit_bytes=56 * 1024 * 1024
        ),
        name="attention",
    )(x, qkv, out_w, gain.reshape(1, width), *weights)


def on_device(
    tokens,
    shifts,
    qkv_weight,
    out_weight,
    up_weight,
    down_weight,
    qk_gain,
    attn_rate,
    mlp_rate,
    hidden_gain,
):
    n_row = lax.axis_size("row")
    n_col = lax.axis_size("col")
    row = lax.axis_index("row")
    local_rows, cols, width = tokens.shape
    local_width = qkv_weight.shape[2]
    hidden = up_weight.shape[1]
    per_window = WIN // cols
    reach = (WIN + cols - 2) // cols
    strip_rows = local_rows * n_row
    count = strip_rows * cols
    shift_row, shift_col = shifts[0], shifts[1]

    gathered = gather_all(
        tokens.reshape(local_rows * cols, width),
        [qkv_weight.reshape(-1, 3 * local_width), out_weight.T],
        n_row,
        n_col,
        reach,
    )
    pieces = gathered[0].reshape(n_row, reach + 1, local_rows, cols, width)
    qkv_full = gathered[1].reshape(width, 3 * local_width)
    out_full = gathered[2].reshape(width, local_width)

    wide = pieces.transpose(0, 2, 1, 3, 4).reshape(strip_rows, (reach + 1) * cols, width)
    strip = lax.dynamic_slice_in_dim(wide, shift_col, cols, axis=1)
    strip = jnp.roll(strip, -shift_row, axis=0).reshape(count, width)
    flat = to_sphere(strip.astype(jnp.float32))
    second = attention(
        flat.astype(jnp.bfloat16),
        qkv_full,
        out_full,
        qk_gain,
        [up_weight, down_weight.T],
        n_row,
        n_col,
        per_window,
        WIN * cols,
    )
    terms = second[0]
    up_full = second[1].reshape(width, hidden)
    down_full = second[2].reshape(width, hidden)
    attn_all = terms[0].astype(jnp.float32)
    for r in range(1, n_row):
        attn_all = attn_all + terms[r].astype(jnp.float32)
    mixed = to_sphere(flat + attn_rate * (to_sphere(attn_all) - flat))

    def feed_forward(rows):
        raised = jnp.dot(rows, up_full, preferred_element_type=jnp.float32)
        activated = jax.nn.gelu(raised * hidden_gain, approximate=False).astype(jnp.bfloat16)
        return lax.dot_general(
            activated, down_full, (((1,), (1,)), ((), ())), preferred_element_type=jnp.float32
        ).astype(jnp.bfloat16)

    def part(value, owner):
        lifted = value.reshape(strip_rows, cols, width)
        twice = jnp.concatenate([lifted, lifted], axis=0)
        first = jnp.mod(owner * local_rows - shift_row, strip_rows)
        return lax.dynamic_slice_in_dim(twice, first, local_rows, 0)

    mixed_bf = mixed.astype(jnp.bfloat16)
    own = part(mixed_bf, row).reshape(local_rows * cols, width)
    moved = []
    for r in range(1, n_row):
        there = feed_forward(part(mixed_bf, lax.rem(row + r, n_row)).reshape(own.shape))
        own, there = lax.optimization_barrier((own, there))
        moved.append(shifted(there, "row", r))
    mlp_local = feed_forward(own).astype(jnp.float32)
    for arrived in moved:
        mlp_local = mlp_local + arrived.astype(jnp.float32)
    mlp_local = mlp_local.reshape(local_rows, cols, width)
    mixed_local = part(mixed, row)
    result = to_sphere(mixed_local + mlp_rate * (to_sphere(mlp_local) - mixed_local))
    result = result.astype(jnp.bfloat16)
    spread = [shifted(result, "col", k) for k in range(reach, 0, -1)] + [result]
    spread = jnp.concatenate(spread, axis=1)
    return lax.dynamic_slice_in_dim(spread, reach * cols - shift_col, cols, axis=1)


def solution(mesh):
    return jax.shard_map(
        on_device,
        mesh=mesh,
        in_specs=(
            P("row", "col", None),
            P(),
            P("col", None, "row"),
            P("row", "col"),
            P("col", "row"),
            P("row", "col"),
            P("row"),
            P(),
            P(),
            P("row"),
        ),
        out_specs=P("row", "col", None),
        check_vma=False,
    )
```

profile of v0, /device:TPU:0, one launch (start us, length us, event | category | flops | bytes accessed | tf_op | source)
XLA Modules:
  0.0 189.3 jit_solution(17597819534605262658)
XLA Ops:
  0.0 1.4 fusion.173
  5.4 0.9 copy.15
  6.4 1.0 copy-done.1
  7.4 0.8 copy-done.2
  8.3 49.6 %gather_all.1 = (bf16[2,3,256,1024]{3,2,1,0:T(8,128)(2,1)S(1)}, bf16[16,64,1536]{2,1,0:T(8,128)(2,1)}, bf16[16,64,512]{2,1,0:T(8,128)(2,1)S(1)}) custom-call(bf16[256,1024]{1,0:T(8,128)(2,1)S(1)} %bitcast.54, bf16[64,1536]{1,0:T(8,128)(2,1)S(1)} %bitcast.53, bf16[64,512]{1,0:T(8,128)(2,1)S(1)} %bitcast.55), custom_call_target="tpu_custom_call" | custom-call | tf_op jit(solution)/shard_map/gather_all/pallas_call | solution.py:139
  57.9 1.0 copy-done
  58.8 0.3 copy.14
  59.9 0.5 constant_dynamic-slice_fusion
  60.3 0.6 fusion.3
  61.1 1.2 fusion.5.refs_0_
  62.3 60.1 %attention.1 = (bf16[2,512,1024]{2,1,0:T(8,128)(2,1)}, bf16[16,64,2048]{2,1,0:T(8,128)(2,1)}, bf16[16,64,2048]{2,1,0:T(8,128)(2,1)}) custom-call(bf16[512,1024]{1,0:T(8,128)(2,1)} %fusion.5.refs_0_, bf16[1024,1536]{1,0:T(8,128)(2,1)} %bitcast.57, bf16[1024,512]{1,0:T(8,128)(2,1)} %bitcast.52, f32[1,512]{1,0:T(1,128)} %bitcast.60, bf16[64,2048]{1,0:T(8,128)(2,1)} %refs_4_.1, ...), custom_call_target="tpu_custom_call" | custom-call | tf_op jit(solution)/shard_map/attention/pallas_call | solution.py:263
  122.4 2.1 %multiply_reduce_fusion.1 = f32[512]{0:T(512)S(1)} fusion(bf16[2,512,1024]{2,1,0:T(8,128)(2,1)} %get-tuple-element.16), kind=kLoop, calls=%fused_computation.55 | loop fusion | flops 2620928 | bytes 2099200 | tf_op jit(solution)/shard_map/reduce_sum | solution.py:24
  124.6 0.9 multiply_reduce_fusion
  125.6 2.5 %fusion.171 = (bf16[64,8,1024]{2,1,0:T(8,128)(2,1)}, f32[64,8,1024]{2,1,0:T(8,128)}) fusion(f32[64,8]{1,0:T(8,128)S(1)} %add_rsqrt_fusion, f32[64,8]{1,0:T(8,128)S(1)} %rsqrt.53, bf16[2,512,1024]{2,1,0:T(8,128)(2,1)S(1)} %copy-done.3, f32[1024]{0:T(1024)S(1)} %copy-done.5, f32[64,8]{1,0:T(8,128)S(1)} %add_rsqrt_fusion.1, ...), kind=kLoop, calls=%fused_computation.214 | loop fusion | flops 5767168 | bytes 6301696 | tf_op jit(solution)/shard_map/convert_element_type | solution.py:357
  128.1 2.1 %fusion.105 = bf16[256,1024]{1,0:T(8,128)(2,1)} fusion(s32[]{:T(128)S(6)} %select_n.42, bf16[64,8,1024]{2,1,0:T(8,128)(2,1)} %get-tuple-element.23), kind=kLoop, calls=%fused_computation.145 | loop fusion | flops 262144 | bytes 1572868 | tf_op jit(solution)/shard_map/reshape | solution.py:358
  130.1 10.3 %convolution_convert_fusion.1 = bf16[256,1024]{1,0:T(8,128)(2,1)S(1)} fusion(bf16[1024,2048]{1,0:T(8,128)(2,1)} %bitcast.63, bf16[1024,2048]{1,0:T(8,128)(2,1)} %bitcast.61, f32[2048]{0:T(1024)S(1)} %copy-done.7, s32[]{:T(128)S(6)} %select_n.44, bf16[64,8,1024]{2,1,0:T(8,128)(2,1)} %get-tuple-element.23), kind=kOutput, calls=%fused_computation.66 | convolution fusion | flops 2182610944 | bytes 9969668 | tf_op jit(solution)/shard_map/dot_general | solution.py:347
  140.5 1.5 collective-permute-start
  142.0 12.9 %collective-permute-done = bf16[256,1024]{1,0:T(8,128)(2,1)} collective-permute-done((bf16[256,1024]{1,0:T(8,128)(2,1)S(1)}, bf16[256,1024]{1,0:T(8,128)(2,1)}, u32[]{:S(2)}, u32[]{:S(2)}) %collective-permute-start) | collective-permute-done | bytes 524320 | tf_op jit(solution)/shard_map/ppermute | solution.py:20
  154.9 10.6 %multiply_reduce_fusion.3 = (f32[256]{0:T(256)S(1)}, f32[256,1024]{1,0:T(8,128)S(1)}) fusion(bf16[256,1024]{1,0:T(8,128)(2,1)} %collective-permute-done, bf16[1024,2048]{1,0:T(8,128)(2,1)} %bitcast.64, bf16[256,1024]{1,0:T(8,128)(2,1)} %fusion.105, bf16[1024,2048]{1,0:T(8,128)(2,1)} %bitcast.62, f32[2048]{0:T(1024)S(1)} %copy-done.7), kind=kOutput, calls=%fused_computation.75 | convolution fusion | flops 2183659264 | bytes 10494976 | tf_op jit(solution)/shard_map/dot_general | solution.py:347
  165.6 0.5 multiply_reduce_fusion.2
  166.1 0.1 multiply_convert_fusion
  167.7 16.0 %collective-permute-done.1 = bf16[32,8,1024]{2,1,0:T(8,128)(2,1)S(1)} collective-permute-done((bf16[32,8,1024]{2,1,0:T(8,128)(2,1)S(1)}, bf16[32,8,1024]{2,1,0:T(8,128)(2,1)S(1)}, u32[]{:S(2)}, u32[]{:S(2)}) %collective-permute-start.1) | collective-permute-done | bytes 524320 | tf_op jit(solution)/shard_map/ppermute | solution.py:20
  183.8 4.2 %collective-permute-done.2 = bf16[32,8,1024]{2,1,0:T(8,128)(2,1)S(1)} collective-permute-done((bf16[32,8,1024]{2,1,0:T(8,128)(2,1)S(1)}, bf16[32,8,1024]{2,1,0:T(8,128)(2,1)S(1)}, u32[]{:S(2)}, u32[]{:S(2)}) %collective-permute-start.2) | collective-permute-done | bytes 524320 | tf_op jit(solution)/shard_map/ppermute | solution.py:20
  188.0 1.4 fusion.99
  (23 shorter events, 0.5 us)
Async XLA Ops:
  6.4 1.0 copy-start.1
  7.4 0.8 copy-start.2
  57.8 1.0 copy-start
  122.4 2.2 %copy-start.3 = (bf16[2,512,1024]{2,1,0:T(8,128)(2,1)S(1)}, bf16[2,512,1024]{2,1,0:T(8,128)(2,1)}, u32[]{:S(2)}) copy-start(bf16[2,512,1024]{2,1,0:T(8,128)(2,1)} %get-tuple-element.16) | copy-start | bytes 6291460
  122.4 2.2 %copy-start.5 = (f32[1024]{0:T(1024)S(1)}, f32[1024]{0:T(1024)}, u32[]{:S(2)}) copy-start(f32[1024]{0:T(1024)} %param.17) | copy-start | bytes 12292
  125.5 4.6 %copy-start.7 = (f32[2048]{0:T(1024)S(1)}, f32[2048]{0:T(1024)}, u32[]{:S(2)}) copy-start(f32[2048]{0:T(1024)} %param.19) | copy-start | bytes 24580
  140.5 25.1 %copy-start.4 = (f32[64,8,1024]{2,1,0:T(8,128)S(1)}, f32[64,8,1024]{2,1,0:T(8,128)}, u32[]{:S(2)}) copy-start(f32[64,8,1024]{2,1,0:T(8,128)} %get-tuple-element.24) | copy-start | bytes 6291460
  140.5 25.1 %copy-start.6 = (f32[1024]{0:T(1024)S(1)}, f32[1024]{0:T(1024)}, u32[]{:S(2)}) copy-start(f32[1024]{0:T(1024)} %param.18) | copy-start | bytes 12292
  140.5 14.4 %collective-permute-start = (bf16[256,1024]{1,0:T(8,128)(2,1)S(1)}, bf16[256,1024]{1,0:T(8,128)(2,1)}, u32[]{:S(2)}, u32[]{:S(2)}) collective-permute-start(bf16[256,1024]{1,0:T(8,128)(2,1)S(1)} %convolution_convert_fusion.1), channel_id=1, source_target_pairs={{0,16},{16,0},{1,17},{17,1},{2,18},{18,2},{3,19},{19,3},{4,20},{20... | collective-permute-start | bytes 1572872 | tf_op jit(solution)/shard_map/ppermute | solution.py:20
  166.2 17.5 %collective-permute-start.1 = (bf16[32,8,1024]{2,1,0:T(8,128)(2,1)S(1)}, bf16[32,8,1024]{2,1,0:T(8,128)(2,1)S(1)}, u32[]{:S(2)}, u32[]{:S(2)}) collective-permute-start(bf16[32,8,1024]{2,1,0:T(8,128)(2,1)S(1)} %multiply_convert_fusion), channel_id=1, source_target_pairs={{0,2},{1,3},{2,4},{3,5},{4,6},{5,7},{6,8},{7,9},{8,10},{9,11},{10,... | collective-permute-start | bytes 1572872 | tf_op jit(solution)/shard_map/ppermute | solution.py:20
  166.3 21.7 %collective-permute-start.2 = (bf16[32,8,1024]{2,1,0:T(8,128)(2,1)S(1)}, bf16[32,8,1024]{2,1,0:T(8,128)(2,1)S(1)}, u32[]{:S(2)}, u32[]{:S(2)}) collective-permute-start(bf16[32,8,1024]{2,1,0:T(8,128)(2,1)S(1)} %multiply_convert_fusion), channel_id=1, source_target_pairs={{0,1},{1,2},{2,3},{3,4},{4,5},{5,6},{6,7},{7,8},{8,9},{9,10},{10,1... | collective-permute-start | bytes 1572872 | tf_op jit(solution)/shard_map/ppermute | solution.py:20
where the time goes:
time: 190 us; the launch traced here: 189 us
  Pallas kernels  110 us (58%)
  waiting for transfers between devices  33.1 us (17%)
  matrix products  20.9 us (11%)
  other arithmetic  11.4 us (6%)
  between operations  6.29 us (3%)
  local copies, waits for them, and re-layouts  6.26 us (3%)
    pallas_call x1, Pallas kernels, attention(): pl.pallas_call(functools.partial(attention_kernel, n_row, n_col, per_wind...  60.1 us
    pallas_call x1, Pallas kernels, gather_all(): pl.pallas_call(functools.partial(gather_kernel, n_row, n_col, reach, n_we...  49.6 us
    ppermute x3, waiting for transfers between devices, shifted(): return lax.ppermute(value, axis, pairs)  33.1 us
    dot_general x2, matrix products, feed_forward(): lax.dot_general(activated, down_full, (((1,), (1,)), ((), ())), preferred...  20.9 us
    reduce_sum x4, other arithmetic, to_sphere(): jnp.mean(vector * vector, axis=-1, keepdims=True) + 1e-06  4.08 us
  transfers between devices with their start and end apart: 3, of which 3 were waited for; matrix products, arithmetic and copies ran while one was open for 0% of the time, Pallas kernels for 0%

commit v1 on v0

v1 whole, which is shorter than its diff:
```python
import functools
import math

import jax
import jax.numpy as jnp
from jax import lax
from jax.experimental import pallas as pl
from jax.experimental.pallas import tpu as pltpu
from jax.sharding import PartitionSpec as P

HD = 64
WIN = 16
LANES = 128
EPS = 1e-06
BF = jnp.bfloat16
F32 = jnp.float32
MESH = pl.DeviceIdType.MESH
VMEM = pl.BlockSpec(memory_space=pltpu.VMEM)
ANY = pl.BlockSpec(memory_space=pl.ANY)
SMEM = pl.BlockSpec(memory_space=pltpu.SMEM)
LAST = (((1,), (1,)), ((), ()))


def to_sphere(vector):
    return vector * lax.rsqrt(jnp.mean(vector * vector, axis=-1, keepdims=True) + EPS)


class Links:
    def __init__(self, n_row, n_col, send_sem, recv_sem):
        self.n_row, self.n_col, self.nz = n_row, n_col, n_col // 4
        self.send_sem, self.recv_sem = send_sem, recv_sem
        self.row, self.col = lax.axis_index("row"), lax.axis_index("col")
        self.z, self.y, self.core = self.col // 4, (self.col // 2) % 2, self.col % 2
        self.z_next = (self.row, self.at(self.z + 1, self.y, self.core))
        self.z_prev = (self.row, self.at(self.z - 1, self.y, self.core))
        self.y_peer = (self.row, self.at(self.z, 1 - self.y, self.core))
        self.core_peer = (self.row, self.at(self.z, self.y, 1 - self.core))
        self.after = (self.row, lax.rem(self.col + 1, n_col))
        self.before = (self.row, lax.rem(self.col + n_col - 1, n_col))
        self.started = []

    def at(self, z, y, core):
        return (lax.rem(z + 2 * self.nz, self.nz) * 2 + y) * 2 + core

    def other_row(self, r):
        return (lax.rem(self.row + r, self.n_row), self.col)

    def greet(self, more):
        peers = [self.z_next, self.z_prev, self.y_peer, self.core_peer, self.after, self.before]
        peers += more + [self.other_row(r) for r in range(1, self.n_row)]
        barrier = pltpu.get_barrier_semaphore()
        for peer in peers:
            pl.semaphore_signal(barrier, inc=1, device_id=peer, device_id_type=MESH)
        pl.semaphore_wait(barrier, len(peers))

    def send(self, src, dst, peer):
        index = len(self.started)
        copy = pltpu.make_async_remote_copy(
            src_ref=src,
            dst_ref=dst,
            send_sem=self.send_sem.at[index],
            recv_sem=self.recv_sem.at[index],
            device_id=peer,
            device_id_type=MESH,
        )
        copy.start()
        self.started.append(copy)
        return copy


class Ring:
    def __init__(self, links, full, depth, low, size, relief):
        self.links, self.full, self.depth, self.low, self.size = links, full, depth, low, size
        self.relief = relief and links.nz > 1
        self.z_copy, self.y_copy, self.core_copy = {}, {}, {}

    def block(self, z, y):
        owner = self.links.at(z, y, self.links.core)
        start = pl.multiple_of(owner * self.depth + self.low, self.size)
        return self.full.at[pl.ds(start, self.size)]

    def to_core(self, name, block):
        self.core_copy[name] = self.links.send(block, block, self.links.core_peer)

    def begin(self):
        links = self.links
        own = self.block(links.z, links.y)
        self.z_copy[0] = links.send(own, own, links.z_next)
        self.y_copy[0] = links.send(own, own, links.y_peer)
        self.to_core(("z", 0), own)

    def along(self, t):
        links = self.links
        self.z_copy[t - 1].wait_recv()
        block = self.block(links.z - t, links.y)
        if t < links.nz - 1:
            self.z_copy[t] = links.send(block, block, links.z_next)
        if not (self.relief and t == 1):
            self.y_copy[t] = links.send(block, block, links.y_peer)
        self.to_core(("z", t), block)

    def across(self, t):
        links = self.links
        block = self.block(links.z - t, 1 - links.y)
        if self.relief and t == 1:
            self.extra.wait_recv()
        else:
            self.y_copy[t].wait_recv()
            if self.relief and t == 0:
                self.extra = links.send(block, block, links.z_next)
        self.to_core(("y", t), block)

    def arrive(self, t):
        self.core_copy["z", t].wait_recv()
        self.core_copy["y", t].wait_recv()

    def arrive_all(self):
        for t in range(self.links.nz):
            self.arrive(t)


def layer_kernel(n_row, n_col, dims, *refs):
    local_rows, cols, depth, width, hidden = dims
    shifts, tok_in, q_in, o_in, u_in, d_in, gain, attn_rate, mlp_rate, hidden_gain, out = refs[:11]
    q_full, o_full, u_full, d_full, o_raw, d_raw, tok, sphere, piece = refs[11:20]
    strip, q_all, kv_all, back, part_send, part_recv, part_own = refs[20:27]
    mixed, mixed_all, active, down_send, down_recv, down_own = refs[27:33]
    local_sem, send_sem, recv_sem, kv_send, kv_recv, back_send, back_recv = refs[33:]

    links = Links(n_row, n_col, send_sem, recv_sem)
    row, col, nz = links.row, links.col, links.nz
    own = local_rows * cols
    rows = local_rows * n_row
    band = WIN * cols
    bands = rows // WIN
    per_window = WIN // cols
    share = depth // n_col
    seat = lax.rem(col, per_window)
    shift_row, shift_col = shifts[0], shifts[1]
    first = jnp.where(shift_col < cols, shift_col + cols, shift_col + cols - WIN)

    def mate(k):
        return (row, col - seat + lax.rem(seat + k, per_window))

    here = pl.ds(pl.multiple_of(col * share, share), share)
    local = [
        pltpu.make_async_copy(src, dst, local_sem.at[i])
        for i, (src, dst) in enumerate(
            [
                (q_in, q_full.at[here]),
                (tok_in, tok),
                (o_in, o_raw),
                (u_in, u_full.at[here]),
                (d_in, d_raw),
            ]
        )
    ]
    for copy in local:
        copy.start()
    links.greet([mate(k) for k in range(1, per_window)])

    half = share // 2
    q_a, q_b = [Ring(links, q_full, share, k * half, half, True) for k in range(2)]
    o_a = Ring(links, o_full, share, 0, share, False)
    u_a, u_b = [Ring(links, u_full, share, k * half, half, True) for k in range(2)]
    d_a, d_b = [Ring(links, d_full, share, k * half, half, True) for k in range(2)]

    local[0].wait()
    q_a.begin()
    q_b.begin()

    chunk = band
    steps = own // chunk
    local[1].wait()
    halo = []
    for i in range(steps):
        part = slice(i * chunk, (i + 1) * chunk)
        value = to_sphere(tok[part, :].astype(F32))
        sphere[part, :] = value
        piece[1, part, :] = value.astype(BF)
        halo.append(
            (
                links.send(piece.at[1, part], piece.at[2, part], links.before),
                links.send(piece.at[1, part], piece.at[0, part], links.after),
            )
        )

    eye = (
        lax.broadcasted_iota(jnp.int32, (share, share), 0)
        == lax.broadcasted_iota(jnp.int32, (share, share), 1)
    ).astype(F32).astype(BF)
    local[2].wait()
    o_full[here, :] = lax.dot_general(eye, o_raw[...], LAST, preferred_element_type=F32).astype(BF)
    o_a.begin()
    q_a.across(0)
    q_a.along(1)
    q_b.across(0)
    q_b.along(1)
    o_a.across(0)
    o_a.along(1)
    local[4].wait()
    d_full[here, :] = lax.dot_general(eye, d_raw[...], LAST, preferred_element_type=F32).astype(BF)

    bits = cols.bit_length() - 1

    def one_hot(length, row_step, column_step, per_piece):
        token = lax.broadcasted_iota(jnp.int32, (band, length), 0)
        source = lax.broadcasted_iota(jnp.int32, (band, length), 1)
        which = lax.shift_right_logical(source, per_piece.bit_length() - 1)
        source = source & (per_piece - 1)
        same_row = lax.shift_right_logical(source, bits) == (
            lax.shift_right_logical(token, bits) + row_step
        )
        same_column = which * cols + (source & (cols - 1)) == (token & (cols - 1)) + column_step
        return jnp.where(same_row & same_column, 1.0, 0.0).astype(BF)

    to_columns = one_hot(3 * band, 0, first, band)
    to_rows = one_hot(2 * band, shift_row, 0, 2 * band)
    to_home = one_hot(6 * band, WIN - shift_row, 2 * cols - first, 2 * band)

    q_a.along(2)
    q_b.along(2)
    local[3].wait()
    u_a.begin()
    u_b.begin()

    spread = []
    for i in range(steps):
        part = slice(i * chunk, (i + 1) * chunk)
        for copy in halo[i]:
            copy.wait_recv()
        near = jnp.concatenate([piece[k, part, :] for k in range(3)], axis=0)
        strip[0, part, :] = jnp.dot(to_columns, near, preferred_element_type=F32).astype(BF)
        spread.append(
            [
                links.send(strip.at[0, part], strip.at[r, part], links.other_row(r))
                for r in range(1, n_row)
            ]
        )
    q_a.across(1)
    q_b.across(1)
    for t in range(3, nz):
        q_a.along(t)
        q_b.along(t)
    for t in range(2, nz):
        q_a.across(t)
        q_b.across(t)
    o_a.along(2)
    o_a.across(1)

    for sent in spread:
        for copy in sent:
            copy.wait_recv()
    q_a.arrive_all()
    q_b.arrive_all()
    group = (lax.broadcasted_iota(jnp.int32, (LANES, LANES), 0) < HD) == (
        lax.broadcasted_iota(jnp.int32, (LANES, LANES), 1) < HD
    )
    averaging = jnp.where(group, 1.0 / HD, 0.0).astype(BF)

    def band_rows(b):
        return pl.ds(pl.multiple_of(b * band, band), band)

    def kv_copy(b, k):
        return pltpu.make_async_remote_copy(
            src_ref=kv_all.at[0, :, band_rows(b)],
            dst_ref=kv_all.at[k, :, band_rows(b)],
            send_sem=kv_send.at[b, k],
            recv_sem=kv_recv.at[b, k],
            device_id=mate(k),
            device_id_type=MESH,
        )

    def back_copy(b, k):
        return pltpu.make_async_remote_copy(
            src_ref=back.at[1, band_rows(b)],
            dst_ref=back.at[2 - 2 * k, band_rows(b)],
            send_sem=back_send.at[b, k],
            recv_sem=back_recv.at[b, k],
            device_id=(links.before, links.after)[k],
            device_id_type=MESH,
        )

    def block_of(b):
        slot = lax.rem(row - b // steps + n_row, n_row)
        return strip[slot, pl.ds(pl.multiple_of(lax.rem(b, steps) * band, band), band), :]

    def project(b, carry):
        near = jnp.concatenate([block_of(b), block_of(lax.rem(b + 1, bands))], axis=0)
        x = jnp.dot(to_rows, near, preferred_element_type=F32).astype(BF)
        for part in range(3):
            got = jnp.dot(
                x, q_full[:, part * width : (part + 1) * width], preferred_element_type=F32
            )
            if part == 2:
                kv_all[0, 1, band_rows(b), :] = got.astype(BF)
                continue
            for lo in range(0, width, LANES):
                cut = slice(lo, lo + LANES)
                one = got[:, cut]
                mean = jnp.dot((one * one).astype(BF), averaging, preferred_element_type=F32)
                scaled = one * lax.rsqrt(mean + EPS) * gain[:, cut]
                if part == 0:
                    q_all[band_rows(b), cut] = (scaled * (1.0 / math.sqrt(HD))).astype(BF)
                else:
                    kv_all[0, 0, band_rows(b), cut] = scaled.astype(BF)
        for k in range(1, per_window):
            kv_copy(b, k).start()
        return carry

    lax.fori_loop(0, bands, project, 0)
    u_a.across(0)
    u_a.along(1)
    u_b.across(0)
    u_b.along(1)
    for t in range(3, nz):
        o_a.along(t)
    for t in range(2, nz):
        o_a.across(t)

    lane = lax.broadcasted_iota(jnp.int32, (band, LANES), 1) < HD

    def attend(b, carry):
        for k in range(1, per_window):
            kv_copy(b, k).wait_recv()
        for lo in range(0, width, LANES):
            cut = slice(lo, lo + LANES)
            query = q_all[band_rows(b), cut].astype(F32)
            both = jnp.concatenate(
                [jnp.where(lane, query, 0.0), jnp.where(lane, 0.0, query)], axis=0
            ).astype(BF)
            keys = jnp.concatenate(
                [kv_all[k, 0, band_rows(b), cut] for k in range(per_window)], axis=0
            )
            values = jnp.concatenate(
                [kv_all[k, 1, band_rows(b), cut] for k in range(per_window)], axis=0
            )
            scores = lax.dot_general(both, keys, LAST, preferred_element_type=F32)
            expo = jnp.exp(scores)
            total = jnp.sum(expo, axis=-1, keepdims=True)
            got = jnp.dot(expo.astype(BF), values, preferred_element_type=F32) / total
            got = jnp.where(lane, got[:band], got[band:]).astype(BF)
            back[1, band_rows(b), cut] = got
        for k in range(2):
            back_copy(b, k).start()
        return carry

    middle = bands // 2
    lax.fori_loop(0, middle, attend, 0)
    u_a.across(1)
    u_b.across(1)
    if nz > 2:
        u_a.along(2)
        u_b.along(2)
    lax.fori_loop(middle, bands, attend, 0)
    for t in range(3, nz):
        u_a.along(t)
        u_b.along(t)
    d_a.begin()
    d_b.begin()
    for t in range(2, nz):
        u_a.across(t)
        u_b.across(t)
    d_a.across(0)
    d_b.across(0)
    d_a.along(1)
    d_b.along(1)

    def returned(b, carry):
        for k in range(2):
            back_copy(b, k).wait_recv()
        return carry

    lax.fori_loop(0, bands, returned, 0)
    o_a.arrive_all()

    def projected_out(owner, i):
        b = owner * steps + i
        earlier = lax.rem(b + bands - 1, bands)
        near = jnp.concatenate(
            [back[k, band_rows(at), :] for k in range(3) for at in (earlier, b)], axis=0
        )
        value = jnp.dot(to_home, near, preferred_element_type=F32).astype(BF)
        return lax.dot_general(value, o_full[...], LAST, preferred_element_type=F32)

    reduced = {}
    for i in range(steps):
        part = slice(i * chunk, (i + 1) * chunk)
        for r in range(1, n_row):
            part_send[r, part, :] = projected_out(lax.rem(row + r, n_row), i).astype(BF)
            reduced[i, r] = links.send(
                part_send.at[r, part], part_recv.at[r, part], links.other_row(r)
            )
    for i in range(steps):
        part_own[i * chunk : (i + 1) * chunk, :] = projected_out(row, i)

    d_a.across(1)
    d_b.across(1)
    if nz > 2:
        d_a.along(2)
        d_b.along(2)
    gathered = {}
    for i in range(steps):
        part = slice(i * chunk, (i + 1) * chunk)
        total = part_own[part, :]
        for r in range(1, n_row):
            reduced[i, r].wait_recv()
            total = total + part_recv[r, part, :].astype(F32)
        base = sphere[part, :]
        value = to_sphere(base + attn_rate[...] * (to_sphere(total) - base))
        mixed[part, :] = value
        mixed_all[0, part, :] = value.astype(BF)
        for r in range(1, n_row):
            gathered[i, r] = links.send(
                mixed_all.at[0, part], mixed_all.at[r, part], links.other_row(r)
            )
    for t in range(3, nz):
        d_a.along(t)
        d_b.along(t)

    u_a.arrive_all()
    u_b.arrive_all()
    tile = min(512, hidden)

    def raise_slot(r):
        def raise_tile(i, carry):
            cut = pl.ds(pl.multiple_of(i * tile, tile), tile)
            raised = jnp.dot(mixed_all[r], u_full[:, cut], preferred_element_type=F32)
            raised = raised * hidden_gain[:, cut]
            active[r, :, cut] = (
                0.5 * raised * (1.0 + lax.erf(raised * (1.0 / math.sqrt(2.0))))
            ).astype(BF)
            return carry

        lax.fori_loop(0, hidden // tile, raise_tile, 0)

    raise_slot(0)
    for t in range(2, nz):
        d_a.across(t)
        d_b.across(t)
    for r in range(1, n_row):
        for i in range(steps):
            gathered[i, r].wait_recv()
        raise_slot(r)

    span = 4 * share
    lowered = {}
    for t in range(nz):
        d_a.arrive(t)
        d_b.arrive(t)
        z = lax.rem(links.z - t + nz, nz)
        weight = d_full[pl.ds(pl.multiple_of(z * span, span), span), :]
        for r in list(range(1, n_row)) + [0]:
            got = lax.dot_general(active[r], weight, LAST, preferred_element_type=F32)
            if r == 0:
                down_own[z] = got
            else:
                down_send[r, z] = got.astype(BF)
                lowered[t, r] = links.send(
                    down_send.at[r, z], down_recv.at[r, z], links.other_row(n_row - r)
                )
    for copy in lowered.values():
        copy.wait_recv()
    for i in range(steps):
        part = slice(i * chunk, (i + 1) * chunk)
        pieces = []
        for z in range(nz):
            total = down_own[z, part, :]
            for r in range(1, n_row):
                total = total + down_recv[r, z, part, :].astype(F32)
            pieces.append(total)
        base = mixed[part, :]
        total = to_sphere(jnp.concatenate(pieces, axis=1))
        out[part, :] = to_sphere(base + mlp_rate[...] * (total - base)).astype(BF)

    for copy in links.started:
        copy.wait_send()

    def drain(b, carry):
        for k in range(1, per_window):
            kv_copy(b, k).wait_send()
        for k in range(2):
            back_copy(b, k).wait_send()
        return carry

    lax.fori_loop(0, bands, drain, 0)


def on_device(
    tokens,
    shifts,
    qkv_weight,
    out_weight,
    up_weight,
    down_weight,
    qk_gain,
    attn_rate,
    mlp_rate,
    hidden_gain,
):
    n_row = lax.axis_size("row")
    n_col = lax.axis_size("col")
    local_rows, cols, depth = tokens.shape
    width = qkv_weight.shape[2]
    hidden = up_weight.shape[1]
    own = local_rows * cols
    rows = local_rows * n_row
    count = rows * cols
    bands = rows // WIN
    per_window = WIN // cols
    share = depth // n_col
    nz = n_col // 4
    span = 4 * share
    steps = own // (WIN * cols)
    copies = 7 * 4 * nz + steps * (2 + 3 * (n_row - 1)) + nz * (n_row - 1)
    dma = pltpu.SemaphoreType.DMA
    result = pl.pallas_call(
        functools.partial(layer_kernel, n_row, n_col, (local_rows, cols, depth, width, hidden)),
        out_shape=jax.ShapeDtypeStruct((own, depth), BF),
        in_specs=[SMEM] + [ANY] * 5 + [VMEM] * 4,
        out_specs=VMEM,
        scratch_shapes=[
            pltpu.VMEM((depth, 3 * width), BF),
            pltpu.VMEM((depth, width), BF),
            pltpu.VMEM((depth, hidden), BF),
            pltpu.VMEM((depth, hidden), BF),
            pltpu.VMEM((width, share), BF),
            pltpu.VMEM((hidden, share), BF),
            pltpu.VMEM((own, depth), BF),
            pltpu.VMEM((own, depth), F32),
            pltpu.VMEM((3, own, depth), BF),
            pltpu.VMEM((n_row, own, depth), BF),
            pltpu.VMEM((count, width), BF),
            pltpu.VMEM((per_window, 2, count, width), BF),
            pltpu.VMEM((3, count, width), BF),
            pltpu.VMEM((n_row, own, depth), BF),
            pltpu.VMEM((n_row, own, depth), BF),
            pltpu.VMEM((own, depth), F32),
            pltpu.VMEM((own, depth), F32),
            pltpu.VMEM((n_row, own, depth), BF),
            pltpu.VMEM((n_row, own, hidden), BF),
            pltpu.VMEM((n_row, nz, own, span), BF),
            pltpu.VMEM((n_row, nz, own, span), BF),
            pltpu.VMEM((nz, own, span), F32),
            dma((5,)),
            dma((copies,)),
            dma((copies,)),
            dma((bands, per_window)),
            dma((bands, per_window)),
            dma((bands, 2)),
            dma((bands, 2)),
        ],
        compiler_params=pltpu.CompilerParams(
            collective_id=0, has_side_effects=True, vmem_limit_bytes=62 * 1024 * 1024
        ),
        name="layer",
    )(
        shifts,
        tokens.reshape(own, depth),
        qkv_weight.reshape(-1, 3 * width),
        out_weight,
        up_weight,
        down_weight,
        qk_gain.reshape(1, width),
        attn_rate.reshape(1, depth),
        mlp_rate.reshape(1, depth),
        hidden_gain.reshape(1, hidden),
    )
    return result.reshape(local_rows, cols, depth)


def solution(mesh):
    return jax.shard_map(
        on_device,
        mesh=mesh,
        in_specs=(
            P("row", "col", None),
            P(),
            P("col", None, "row"),
            P("row", "col"),
            P("col", "row"),
            P("row", "col"),
            P("row"),
            P(),
            P(),
            P("row"),
        ),
        out_specs=P("row", "col", None),
        check_vma=False,
    )
```

time: 190 us -> 131 us (0.69)
  waiting for transfers between devices: 33.1 us -> 0 us
  matrix products: 20.9 us -> 0 us
  Pallas kernels: 110 us -> 125 us
  other arithmetic: 11.4 us -> 0 us
  between operations: 6.29 us -> 0.01 us
    ppermute x3 -> x0, waiting for transfers between devices: 33.1 us -> none  [shifted(): return lax.ppermute(value, axis, pairs)]
    dot_general x2 -> x0, matrix products: 20.9 us -> none  [feed_forward(): lax.dot_general(activated, down_full, (((1,), (1,)), ((), ())), preferred...]
    pallas_call x2 -> x1, Pallas kernels: 110 us -> 125 us  [on_device(): pl.pallas_call(functools.partial(layer_kernel, n_row, n_col, (local_rows,...]
    reduce_sum x4 -> x0, other arithmetic: 4.08 us -> none  [to_sphere(): jnp.mean(vector * vector, axis=-1, keepdims=True) + 1e-06]
    convert_element_type x3 -> x0, other arithmetic: 3.85 us -> none  [the longest x1 2.51 us: on_device(): mixed_bf = mixed.astype(jnp.bfloat16)]
    reshape x1 -> x0, other arithmetic: 2.07 us -> none  [on_device(): own = part(mixed_bf, row).reshape(local_rows * cols, width)]
    unnamed x16 -> x7, local copies, waits for them, and re-layouts: 2.9 us -> 4.52 us
  transfers between devices with their start and end apart: 3 -> 0, of which waited for: 3 -> 0; matrix products, arithmetic and copies ran while one was open for 0% -> 0% of each run, Pallas kernels for 0% -> 0%
where the time goes in v1:
time: 131 us; the launch traced here: 130 us
  Pallas kernels  125 us (95%)
  local copies, waits for them, and re-layouts  5.2 us (4%)
    pallas_call x1, Pallas kernels, on_device(): pl.pallas_call(functools.partial(layer_kernel, n_row, n_col, (local_rows,...  125 us
    unnamed x7, local copies, waits for them, and re-layouts  4.52 us

profile of v1, /device:TPU:0, one launch (start us, length us, event | category | flops | bytes accessed | tf_op | source)
XLA Modules:
  0.0 129.8 jit_solution(911762970912085935)
XLA Ops:
  0.0 0.0 copy-start.1
  0.0 0.0 copy-start
  0.0 1.6 %copy.15.refs_3_ = bf16[512,64]{1,0:T(8,128)(2,1)} copy(bf16[512,64]{0,1:T(8,128)(2,1)} %param.13) | data formatting | bytes 131072 | tf_op args[3]
  1.6 0.0 copy-done.1
  1.6 0.7 copy.17
  2.3 0.0 copy-done
  2.3 1.0 copy.16.refs_5_
  3.3 124.6 %layer.1 = bf16[256,1024]{1,0:T(8,128)(2,1)} custom-call(s32[2]{0:T(128)} %refs_0_.1, bf16[256,1024]{1,0:T(8,128)(2,1)} %bitcast.10, bf16[64,1536]{1,0:T(8,128)(2,1)} %bitcast.9, bf16[512,64]{1,0:T(8,128)(2,1)} %copy.15.refs_3_, bf16[64,2048]{1,0:T(8,128)(2,1)} %refs_4_.1, bf16[2048,64]{1,0:T(8,128)(2,1)} %copy.16.refs_5_, f32[1,512]{1,0:T(1,128)} %bitcast.15, ...), custom_call_target="tpu_custom_call" | custom-call | tf_op jit(solution)/shard_map/layer/pallas_call | solution.py:517
  127.9 1.9 %copy.19 = bf16[32,8,1024]{2,1,0:T(8,128)(2,1)} copy(bf16[32,8,1024]{2,1,0:T(8,128)(2,1)} %bitcast.8) | data formatting | bytes 1048576
Async XLA Ops:
  0.0 1.6 %copy-start.1 = (bf16[64,3,512]{2,0,1:T(8,128)(2,1)S(1)}, bf16[64,3,512]{2,0,1:T(8,128)(2,1)}, u32[]{:S(2)}) copy-start(bf16[64,3,512]{2,0,1:T(8,128)(2,1)} %param.12) | copy-start | bytes 589828
  0.0 2.3 %copy-start = (bf16[2048,64]{0,1:T(8,128)(2,1)S(1)}, bf16[2048,64]{0,1:T(8,128)(2,1)}, u32[]{:S(2)}) copy-start(bf16[2048,64]{0,1:T(8,128)(2,1)} %param.15) | copy-start | bytes 786436

commit v2 on v1

v2 whole, which is shorter than its diff:
```python
import functools
import math

import jax
import jax.numpy as jnp
from jax import lax
from jax.experimental import pallas as pl
from jax.experimental.pallas import tpu as pltpu
from jax.sharding import PartitionSpec as P

HD = 64
WIN = 16
LANES = 128
EPS = 1e-06
BF = jnp.bfloat16
F32 = jnp.float32
MESH = pl.DeviceIdType.MESH
VMEM = pl.BlockSpec(memory_space=pltpu.VMEM)
ANY = pl.BlockSpec(memory_space=pl.ANY)
SMEM = pl.BlockSpec(memory_space=pltpu.SMEM)
LAST = (((1,), (1,)), ((), ()))


def to_sphere(vector):
    return vector * lax.rsqrt(jnp.mean(vector * vector, axis=-1, keepdims=True) + EPS)


class Links:
    def __init__(self, n_row, n_col, send_sem, recv_sem):
        self.n_row, self.n_col, self.nz = n_row, n_col, n_col // 4
        self.send_sem, self.recv_sem = send_sem, recv_sem
        self.row, self.col = lax.axis_index("row"), lax.axis_index("col")
        self.z, self.y, self.core = self.col // 4, (self.col // 2) % 2, self.col % 2
        self.z_next = (self.row, self.at(self.z + 1, self.y, self.core))
        self.z_prev = (self.row, self.at(self.z - 1, self.y, self.core))
        self.y_peer = (self.row, self.at(self.z, 1 - self.y, self.core))
        self.core_peer = (self.row, self.at(self.z, self.y, 1 - self.core))
        self.after = (self.row, lax.rem(self.col + 1, n_col))
        self.before = (self.row, lax.rem(self.col + n_col - 1, n_col))
        self.started = []

    def at(self, z, y, core):
        return (lax.rem(z + 2 * self.nz, self.nz) * 2 + y) * 2 + core

    def other_row(self, r):
        return (lax.rem(self.row + r, self.n_row), self.col)

    def greet(self, more):
        peers = [self.z_next, self.z_prev, self.y_peer, self.core_peer, self.after, self.before]
        peers += more + [self.other_row(r) for r in range(1, self.n_row)]
        barrier = pltpu.get_barrier_semaphore()
        for peer in peers:
            pl.semaphore_signal(barrier, inc=1, device_id=peer, device_id_type=MESH)
        pl.semaphore_wait(barrier, len(peers))

    def make(self, src, dst, peer):
        index = len(self.started)
        copy = pltpu.make_async_remote_copy(
            src_ref=src,
            dst_ref=dst,
            send_sem=self.send_sem.at[index],
            recv_sem=self.recv_sem.at[index],
            device_id=peer,
            device_id_type=MESH,
        )
        self.started.append(copy)
        return copy

    def send(self, src, dst, peer):
        copy = self.make(src, dst, peer)
        copy.start()
        return copy


class Ring:
    def __init__(self, links, full, depth, low, size, relief, rows=()):
        self.links, self.full, self.depth, self.low, self.size = links, full, depth, low, size
        self.relief = relief and links.nz > 1
        self.rows = rows
        self.z_copy, self.y_copy, self.core_copy, self.row_copy = {}, {}, {}, {}

    def place(self, z, y):
        owner = self.links.at(z, y, self.links.core)
        return pl.ds(pl.multiple_of(owner * self.depth + self.low, self.size), self.size)

    def block(self, z, y):
        return self.full.at[self.place(z, y)]

    def to_core(self, name, block):
        links = self.links
        self.core_copy[name] = links.send(block, block, links.core_peer)
        for r, there in self.rows:
            z = links.z - name[1]
            place = self.place(z, links.y if name[0] == "z" else 1 - links.y)
            self.row_copy[name, r] = links.send(block, there.at[place], links.other_row(r))

    def beyond(self):
        links = self.links
        for t in range(links.nz):
            for kind, y in (("z", links.y), ("y", 1 - links.y)):
                for r, there in self.rows:
                    self.row_copy[(kind, t), r].wait_recv()
                    block = there.at[self.place(links.z - t, y)]
                    self.core_copy[kind, t, r] = links.send(block, block, links.core_peer)

    def begin_z(self):
        own = self.block(self.links.z, self.links.y)
        self.z_copy[0] = self.links.send(own, own, self.links.z_next)
        self.to_core(("z", 0), own)

    def begin_y(self):
        own = self.block(self.links.z, self.links.y)
        self.y_copy[0] = self.links.send(own, own, self.links.y_peer)

    def begin(self):
        self.begin_z()
        self.begin_y()

    def along(self, t):
        links = self.links
        self.z_copy[t - 1].wait_recv()
        block = self.block(links.z - t, links.y)
        if t < links.nz - 1:
            self.z_copy[t] = links.send(block, block, links.z_next)
        if not (self.relief and t == 1):
            self.y_copy[t] = links.send(block, block, links.y_peer)
        self.to_core(("z", t), block)

    def across(self, t):
        links = self.links
        block = self.block(links.z - t, 1 - links.y)
        if self.relief and t == 1:
            self.extra.wait_recv()
        else:
            self.y_copy[t].wait_recv()
            if self.relief and t == 0:
                self.extra = links.send(block, block, links.z_next)
        self.to_core(("y", t), block)

    def arrive(self, t):
        self.core_copy["z", t].wait_recv()
        self.core_copy["y", t].wait_recv()

    def arrive_all(self):
        for copy in self.core_copy.values():
            copy.wait_recv()


def layer_kernel(n_row, n_col, dims, side, *refs):
    local_rows, cols, depth, width, hidden = dims
    shifts, tok_in, q_in, o_in, u_in, d_in, gain, attn_rate, mlp_rate, hidden_gain, out = refs[:11]
    q_full, o_all, u_full, d_full, tok, piece, sphere_all = refs[11:18]
    strip, q_all, kv_all, back, home_all = refs[18:23]
    mixed_all, active, down_send, down_recv, down_own = refs[23:28]
    local_sem, send_sem, recv_sem, kv_send, kv_recv, back_send, back_recv = refs[28:35]
    home_send, home_recv = refs[35:]

    links = Links(n_row, n_col, send_sem, recv_sem)
    row, col, nz = links.row, links.col, links.nz
    own = local_rows * cols
    rows = local_rows * n_row
    band = WIN * cols
    bands = rows // WIN
    per_window = WIN // cols
    share = depth // n_col
    seat = lax.rem(col, per_window)
    shift_row, shift_col = shifts[0], shifts[1]
    mine = 0 if side > 0 else 1
    first = shift_col if side > 0 else shift_col - cols

    def mate(k):
        return (row, col - seat + lax.rem(seat + k, per_window))

    here = pl.ds(pl.multiple_of(col * share, share), share)
    local = [
        pltpu.make_async_copy(src, dst, local_sem.at[i])
        for i, (src, dst) in enumerate(
            [(q_in.at[p], q_full.at[here, pl.ds(p * width, width)]) for p in range(3)]
            + [
                (tok_in, tok),
                (o_in, o_all.at[0, here]),
                (u_in, u_full.at[here]),
                (d_in, d_full.at[here]),
            ]
        )
    ]
    for copy in local:
        copy.start()
    source, target = (links.after, links.before) if side > 0 else (links.before, links.after)
    links.greet([mate(k) for k in range(1, per_window)])

    half = share // 2
    q_a, q_b = [Ring(links, q_full, share, k * half, half, k == 0) for k in range(2)]
    o_rows = [(r, o_all.at[r]) for r in range(1, n_row)]
    o_a = Ring(links, o_all.at[0], share, 0, share, False, o_rows)
    u_a, u_b = [Ring(links, u_full, share, k * half, half, k == 0) for k in range(2)]
    d_a, d_b = [Ring(links, d_full, share, k * half, half, k == 0) for k in range(2)]

    chunk = band
    steps = own // chunk
    local[3].wait()
    halo = []
    for i in range(steps):
        part = slice(i * chunk, (i + 1) * chunk)
        value = to_sphere(tok[part, :].astype(F32)).astype(BF)
        sphere_all[0, part, :] = value
        piece[mine, part, :] = value
        halo.append(links.send(piece.at[mine, part], piece.at[1 - mine, part], target))
    for copy in local[:3]:
        copy.wait()
    q_a.begin()
    q_b.begin()

    bits = cols.bit_length() - 1

    def one_hot(length, row_step, column_step, per_piece):
        token = lax.broadcasted_iota(jnp.int32, (band, length), 0)
        source = lax.broadcasted_iota(jnp.int32, (band, length), 1)
        which = lax.shift_right_logical(source, per_piece.bit_length() - 1)
        source = source & (per_piece - 1)
        same_row = lax.shift_right_logical(source, bits) == (
            lax.shift_right_logical(token, bits) + row_step
        )
        same_column = which * cols + (source & (cols - 1)) == (token & (cols - 1)) + column_step
        return jnp.where(same_row & same_column, 1.0, 0.0).astype(BF)

    to_columns = one_hot(2 * band, 0, first, band)
    to_rows = one_hot(2 * band, shift_row, 0, 2 * band)
    to_home = one_hot(4 * band, WIN - shift_row, cols - first, 2 * band)

    spread = [
        [
            links.make(
                strip.at[0, pl.ds(i * chunk, chunk)],
                strip.at[r, pl.ds(i * chunk, chunk)],
                links.other_row(r),
            )
            for r in range(1, n_row)
        ]
        for i in range(steps)
    ]

    def shift_columns():
        for i in range(steps):
            part = slice(i * chunk, (i + 1) * chunk)
            halo[i].wait_recv()
            near = jnp.concatenate([piece[k, part, :] for k in range(2)], axis=0)
            strip[0, part, :] = jnp.dot(to_columns, near, preferred_element_type=F32).astype(BF)
            for copy in spread[i]:
                copy.start()

    inside = links.core == (0 if side > 0 else 1)
    pl.when(inside)(shift_columns)
    for ring in (q_a, q_b):
        ring.across(0)
        ring.along(1)
    pl.when(jnp.logical_not(inside))(shift_columns)
    local[4].wait()
    o_a.begin()
    q_a.along(2)
    q_a.across(1)
    q_b.along(2)
    q_b.across(1)
    local[5].wait()
    u_a.begin_z()
    for ring in (q_a, q_b):
        for t in range(3, nz):
            ring.along(t)
        ring.across(2)
    u_a.begin_y()
    u_b.begin_z()
    around = [
        links.send(sphere_all.at[0], sphere_all.at[r], links.other_row(r))
        for r in range(1, n_row)
    ]
    o_a.along(1)
    o_a.across(0)
    for ring in (q_a, q_b):
        for t in range(3, nz):
            ring.across(t)
    u_b.begin_y()
    o_a.along(2)
    o_a.across(1)
    u_a.along(1)
    for sent in spread:
        for copy in sent:
            copy.wait_recv()
    q_a.arrive_all()
    q_b.arrive_all()
    group = (lax.broadcasted_iota(jnp.int32, (LANES, LANES), 0) < HD) == (
        lax.broadcasted_iota(jnp.int32, (LANES, LANES), 1) < HD
    )
    averaging = jnp.where(group, 1.0 / HD, 0.0).astype(BF)

    def band_rows(b):
        return pl.ds(pl.multiple_of(b * band, band), band)

    def kv_copy(b, k):
        return pltpu.make_async_remote_copy(
            src_ref=kv_all.at[0, :, band_rows(b)],
            dst_ref=kv_all.at[k, :, band_rows(b)],
            send_sem=kv_send.at[b, k],
            recv_sem=kv_recv.at[b, k],
            device_id=mate(k),
            device_id_type=MESH,
        )

    def back_copy(b):
        return pltpu.make_async_remote_copy(
            src_ref=back.at[1 - mine, band_rows(b)],
            dst_ref=back.at[mine, band_rows(b)],
            send_sem=back_send.at[b],
            recv_sem=back_recv.at[b],
            device_id=source,
            device_id_type=MESH,
        )

    def home_copy(b, r):
        return pltpu.make_async_remote_copy(
            src_ref=home_all.at[0, band_rows(b)],
            dst_ref=home_all.at[r, band_rows(b)],
            send_sem=home_send.at[b, r],
            recv_sem=home_recv.at[b, r],
            device_id=links.other_row(r),
            device_id_type=MESH,
        )

    def block_of(b):
        slot = lax.rem(row - b // steps + n_row, n_row)
        return strip[slot, pl.ds(pl.multiple_of(lax.rem(b, steps) * band, band), band), :]

    def project(b, carry):
        near = jnp.concatenate([block_of(b), block_of(lax.rem(b + 1, bands))], axis=0)
        x = jnp.dot(to_rows, near, preferred_element_type=F32).astype(BF)
        for part in range(3):
            got = jnp.dot(
                x, q_full[:, part * width : (part + 1) * width], preferred_element_type=F32
            )
            if part == 2:
                kv_all[0, 1, band_rows(b), :] = got.astype(BF)
                continue
            for lo in range(0, width, LANES):
                cut = slice(lo, lo + LANES)
                one = got[:, cut]
                mean = jnp.dot((one * one).astype(BF), averaging, preferred_element_type=F32)
                scaled = one * lax.rsqrt(mean + EPS) * gain[:, cut]
                if part == 0:
                    q_all[band_rows(b), cut] = (scaled * (1.0 / math.sqrt(HD))).astype(BF)
                else:
                    kv_all[0, 0, band_rows(b), cut] = scaled.astype(BF)
        for k in range(1, per_window):
            kv_copy(b, k).start()
        return carry

    lane = lax.broadcasted_iota(jnp.int32, (band, LANES), 1) < HD

    def attend(b, carry):
        for k in range(1, per_window):
            kv_copy(b, k).wait_recv()
        for lo in range(0, width, LANES):
            cut = slice(lo, lo + LANES)
            query = q_all[band_rows(b), cut].astype(F32)
            both = jnp.concatenate(
                [jnp.where(lane, query, 0.0), jnp.where(lane, 0.0, query)], axis=0
            ).astype(BF)
            keys = jnp.concatenate(
                [kv_all[k, 0, band_rows(b), cut] for k in range(per_window)], axis=0
            )
            values = jnp.concatenate(
                [kv_all[k, 1, band_rows(b), cut] for k in range(per_window)], axis=0
            )
            scores = lax.dot_general(both, keys, LAST, preferred_element_type=F32)
            expo = jnp.exp(scores)
            total = jnp.sum(expo, axis=-1, keepdims=True)
            got = jnp.dot(expo.astype(BF), values, preferred_element_type=F32) / total
            got = jnp.where(lane, got[:band], got[band:]).astype(BF)
            back[1 - mine, band_rows(b), cut] = got
        back_copy(b).start()
        return carry

    def project_attend(b, carry):
        project(b, 0)
        attend(b - 1, 0)
        return carry

    project(0, 0)
    u_b.along(1)
    u_a.across(0)
    u_b.across(0)
    lax.fori_loop(1, bands, project_attend, 0)
    attend(bands - 1, 0)
    u_a.along(2)
    u_b.along(2)
    for t in range(3, nz):
        o_a.along(t)
    o_a.across(2)
    local[6].wait()
    d_a.begin_z()

    def go_home(j, carry):
        b = lax.rem(j + 1, bands)

        @pl.when(j == 0)
        def _():
            back_copy(0).wait_recv()

        @pl.when(j < bands - 1)
        def _():
            back_copy(b).wait_recv()

        earlier = lax.rem(b + bands - 1, bands)
        near = jnp.concatenate(
            [back[k, band_rows(at), :] for k in range(2) for at in (earlier, b)], axis=0
        )
        home_all[0, band_rows(b), :] = jnp.dot(
            to_home, near, preferred_element_type=F32
        ).astype(BF)
        for r in range(1, n_row):
            home_copy(b, r).start()
        return carry

    lax.fori_loop(0, bands, go_home, 0)
    u_a.across(1)
    u_b.across(1)
    d_b.begin_z()
    for t in range(3, nz):
        o_a.across(t)
    d_a.begin_y()
    d_b.begin_y()
    for ring in (u_a, u_b):
        for t in range(3, nz):
            ring.along(t)
        ring.across(2)
    o_a.beyond()
    o_a.arrive_all()
    for copy in around:
        copy.wait_recv()

    def mix(j, carry):
        b = lax.rem(j + 1, bands)
        slot = lax.rem(row - b // steps + n_row, n_row)
        part = pl.ds(pl.multiple_of(lax.rem(b, steps) * chunk, chunk), chunk)
        total = None
        for r in range(n_row):
            if r > 0:
                home_copy(b, r).wait_recv()
            term = lax.dot_general(
                home_all[r, band_rows(b), :], o_all[r], LAST, preferred_element_type=F32
            )
            total = term if total is None else total + term
        base = sphere_all[slot, part, :].astype(F32)
        value = to_sphere(base + attn_rate[...] * (to_sphere(total) - base))
        mixed_all[slot, part, :] = value.astype(BF)
        return carry

    lax.fori_loop(0, bands, mix, 0)
    d_a.along(1)
    d_b.along(1)
    d_a.across(0)
    d_b.across(0)
    for ring in (u_a, u_b):
        for t in range(3, nz):
            ring.across(t)
    u_a.arrive_all()
    u_b.arrive_all()
    tile = min(512, hidden)

    def raise_slot(r):
        def raise_tile(i, carry):
            cut = pl.ds(pl.multiple_of(i * tile, tile), tile)
            raised = jnp.dot(mixed_all[r], u_full[:, cut], preferred_element_type=F32)
            raised = raised * hidden_gain[:, cut]
            active[r, :, cut] = (
                0.5 * raised * (1.0 + lax.erf(raised * (1.0 / math.sqrt(2.0))))
            ).astype(BF)
            return carry

        lax.fori_loop(0, hidden // tile, raise_tile, 0)

    raise_slot(0)
    for ring in (d_a, d_b):
        ring.along(2)
        ring.across(1)
    for r in range(1, n_row):
        raise_slot(r)
    for ring in (d_a, d_b):
        for t in range(3, nz):
            ring.along(t)
        ring.across(2)

    span = 4 * share
    lowered = {}
    for t in range(nz):
        for ring in (d_a, d_b):
            if t > 2:
                ring.across(t)
            ring.arrive(t)
        z = lax.rem(links.z - t + nz, nz)
        weight = d_full[pl.ds(pl.multiple_of(z * span, span), span), :]
        for r in list(range(1, n_row)) + [0]:
            got = lax.dot_general(active[r], weight, LAST, preferred_element_type=F32)
            if r == 0:
                down_own[z] = got
            else:
                down_send[r, z] = got.astype(BF)
                lowered[t, r] = links.send(
                    down_send.at[r, z], down_recv.at[r, z], links.other_row(n_row - r)
                )
    for copy in lowered.values():
        copy.wait_recv()
    for i in range(steps):
        part = slice(i * chunk, (i + 1) * chunk)
        pieces = []
        for z in range(nz):
            total = down_own[z, part, :]
            for r in range(1, n_row):
                total = total + down_recv[r, z, part, :].astype(F32)
            pieces.append(total)
        base = mixed_all[0, part, :].astype(F32)
        total = to_sphere(jnp.concatenate(pieces, axis=1))
        out[part, :] = to_sphere(base + mlp_rate[...] * (total - base)).astype(BF)

    for copy in links.started:
        copy.wait_send()

    def drain(b, carry):
        for k in range(1, per_window):
            kv_copy(b, k).wait_send()
        back_copy(b).wait_send()
        for r in range(1, n_row):
            home_copy(b, r).wait_send()
        return carry

    lax.fori_loop(0, bands, drain, 0)


def on_device(
    tokens,
    shifts,
    qkv_weight,
    out_weight,
    up_weight,
    down_weight,
    qk_gain,
    attn_rate,
    mlp_rate,
    hidden_gain,
):
    n_row = lax.axis_size("row")
    n_col = lax.axis_size("col")
    local_rows, cols, depth = tokens.shape
    width = qkv_weight.shape[2]
    hidden = up_weight.shape[1]
    own = local_rows * cols
    rows = local_rows * n_row
    count = rows * cols
    bands = rows // WIN
    per_window = WIN // cols
    share = depth // n_col
    nz = n_col // 4
    span = 4 * share
    steps = own // (WIN * cols)
    copies = 7 * 4 * nz + steps * n_row + (n_row - 1) * (5 * nz + 1)
    dma = pltpu.SemaphoreType.DMA
    dims = (local_rows, cols, depth, width, hidden)

    def layer(side, *operands):
        return pl.pallas_call(
        functools.partial(layer_kernel, n_row, n_col, dims, side),
        out_shape=jax.ShapeDtypeStruct((own, depth), BF),
        in_specs=[SMEM] + [ANY] * 5 + [VMEM] * 4,
        out_specs=VMEM,
        scratch_shapes=[
            pltpu.VMEM((depth, 3 * width), BF),
            pltpu.VMEM((n_row, depth, width), BF),
            pltpu.VMEM((depth, hidden), BF),
            pltpu.VMEM((depth, hidden), BF),
            pltpu.VMEM((own, depth), BF),
            pltpu.VMEM((2, own, depth), BF),
            pltpu.VMEM((n_row, own, depth), BF),
            pltpu.VMEM((n_row, own, depth), BF),
            pltpu.VMEM((count, width), BF),
            pltpu.VMEM((per_window, 2, count, width), BF),
            pltpu.VMEM((2, count, width), BF),
            pltpu.VMEM((n_row, count, width), BF),
            pltpu.VMEM((n_row, own, depth), BF),
            pltpu.VMEM((n_row, own, hidden), BF),
            pltpu.VMEM((n_row, nz, own, span), BF),
            pltpu.VMEM((n_row, nz, own, span), BF),
            pltpu.VMEM((nz, own, span), F32),
            dma((7,)),
            dma((copies,)),
            dma((copies,)),
            dma((bands, per_window)),
            dma((bands, per_window)),
            dma((bands,)),
            dma((bands,)),
            dma((bands, n_row)),
            dma((bands, n_row)),
        ],
        compiler_params=pltpu.CompilerParams(
            collective_id=0 if side > 0 else 1, has_side_effects=True, vmem_limit_bytes=62 * 1024 * 1024
        ),
        name="layer",
    )(*operands)

    result = lax.cond(
        shifts[1] < cols,
        functools.partial(layer, 1),
        functools.partial(layer, -1),
        shifts,
        tokens.reshape(own, depth),
        qkv_weight.transpose(1, 0, 2),
        out_weight.T,
        up_weight,
        down_weight.T,
        qk_gain.reshape(1, width),
        attn_rate.reshape(1, depth),
        mlp_rate.reshape(1, depth),
        hidden_gain.reshape(1, hidden),
    )
    return result.reshape(local_rows, cols, depth)


def solution(mesh):
    return jax.shard_map(
        on_device,
        mesh=mesh,
        in_specs=(
            P("row", "col", None),
            P(),
            P("col", None, "row"),
            P("row", "col"),
            P("col", "row"),
            P("row", "col"),
            P("row"),
            P(),
            P(),
            P("row"),
        ),
        out_specs=P("row", "col", None),
        check_vma=False,
    )
```

time: 131 us -> 110 us (0.84)
  Pallas kernels: 125 us -> 104 us
  local copies, waits for them, and re-layouts: 5.2 us -> 3.41 us
    pallas_call x1, Pallas kernels: 125 us -> 104 us  [layer(): pl.pallas_call(functools.partial(layer_kernel, n_row, n_col, dims, side),...]
    unnamed x7, local copies, waits for them, and re-layouts: 4.52 us -> 1.47 us
where the time goes in v2:
time: 110 us; the launch traced here: 109 us
  Pallas kernels  104 us (95%)
  local copies, waits for them, and re-layouts  3.41 us (3%)
    pallas_call x1, Pallas kernels, layer(): pl.pallas_call(functools.partial(layer_kernel, n_row, n_col, dims, side),...  104 us

profile of v2, /device:TPU:0, one launch (start us, length us, event | category | flops | bytes accessed | tf_op | source)
XLA Modules:
  0.0 108.7 jit_solution(6748114126866028161)
XLA Ops:
  0.0 0.0 copy-start
  0.0 1.2 %slice.3 = s32[1]{0:T(128)} slice(s32[2]{0:T(128)} %param.13), slice={[1:2]} | slice | bytes 8 | tf_op jit(solution)/shard_map/slice | solution.py:608
  1.9 0.0 copy-start.1
  1.9 0.0 copy-start.6
  1.9 0.0 copy-done
  1.9 0.7 copy-done.1
  2.6 0.0 copy-done.6
  2.6 105.3 %conditional.1 = (bf16[32,8,1024]{2,1,0:T(8,128)(2,1)S(1)}) conditional(s32[]{:T(128)} %bitcast.12, (s32[2]{0:T(128)S(1)}, bf16[32,8,1024]{2,1,0:T(8,128)(2,1)}, bf16[3,64,512]{2,1,0:T(8,128)(2,1)}, bf16[64,512]{1,0:T(8,128)(2,1)}, bf16[64,2048]{1,0:T(8,128)(2,1)}, /*index=5*/bf16[64,2048]{1,0:T(8,128)(2,1)}, f32[512]{0:T(512)}, f32[1024]{0:T(1024)S(1)}, ...), branch_computations={%region_0.0_spmd, %region_1.0_spmd} | conditional | bytes 24640 | solution.py:607
  2.6 0.0 copy-start.3
  2.6 0.0 copy-start.5
  2.6 0.7 copy-done.3
  3.3 0.0 copy-done.5
  3.3 104.4 %layer.3 = bf16[256,1024]{1,0:T(8,128)(2,1)S(1)} custom-call(s32[2]{0:T(128)S(1)} %get-tuple-element.59.refs_0_, bf16[256,1024]{1,0:T(8,128)(2,1)} %bitcast.17, bf16[3,64,512]{2,1,0:T(8,128)(2,1)} %get-tuple-element.61.refs_2_, bf16[64,512]{1,0:T(8,128)(2,1)} %get-tuple-element.62.refs_3_, bf16[64,2048]{1,0:T(8,128)(2,1)} %get-tuple-element.85.refs_4_, ...), custom_call_target="tpu_custom_call" | custom-call | tf_op jit(solution)/shard_map/cond/branch_1_fun/layer/pallas_call | solution.py:568
  107.9 0.8 copy.28
Async XLA Ops:
  0.0 1.9 %copy-start = (f32[2048]{0:T(1024)S(1)}, f32[2048]{0:T(1024)}, u32[]{:S(2)}) copy-start(f32[2048]{0:T(1024)} %param.21) | copy-start | bytes 24580
  1.9 0.7 copy-start.1
  1.9 0.7 copy-start.6
  2.6 0.7 copy-start.3
  2.6 0.7 copy-start.5

commit v3 on v2

--- a/solution.py
+++ b/solution.py
@@ -26,13 +26,12 @@
 
 
 class Links:
-    def __init__(self, n_row, n_col, send_sem, recv_sem):
+    def __init__(self, n_row, n_col, side, send_sem, recv_sem):
+        self.side = side
         self.n_row, self.n_col, self.nz = n_row, n_col, n_col // 4
         self.send_sem, self.recv_sem = send_sem, recv_sem
         self.row, self.col = lax.axis_index("row"), lax.axis_index("col")
         self.z, self.y, self.core = self.col // 4, (self.col // 2) % 2, self.col % 2
-        self.z_next = (self.row, self.at(self.z + 1, self.y, self.core))
-        self.z_prev = (self.row, self.at(self.z - 1, self.y, self.core))
         self.y_peer = (self.row, self.at(self.z, 1 - self.y, self.core))
         self.core_peer = (self.row, self.at(self.z, self.y, 1 - self.core))
         self.after = (self.row, lax.rem(self.col + 1, n_col))
@@ -42,42 +41,61 @@
     def at(self, z, y, core):
         return (lax.rem(z + 2 * self.nz, self.nz) * 2 + y) * 2 + core
 
+    def along(self, t):
+        return (self.row, self.at(self.z + t, self.y, self.core))
+
+    def turn(self, t):
+        return t if self.side > 0 else (self.nz - t) % self.nz
+
     def other_row(self, r):
         return (lax.rem(self.row + r, self.n_row), self.col)
 
     def greet(self, more):
-        peers = [self.z_next, self.z_prev, self.y_peer, self.core_peer, self.after, self.before]
+        peers = [self.y_peer, self.core_peer, self.after, self.before]
+        peers += [self.along(t) for t in range(1, self.nz)]
         peers += more + [self.other_row(r) for r in range(1, self.n_row)]
         barrier = pltpu.get_barrier_semaphore()
         for peer in peers:
             pl.semaphore_signal(barrier, inc=1, device_id=peer, device_id_type=MESH)
         pl.semaphore_wait(barrier, len(peers))
 
-    def make(self, src, dst, peer):
+    def make(self, src, dst, peer, when=None, landing=None):
         index = len(self.started)
         copy = pltpu.make_async_remote_copy(
             src_ref=src,
             dst_ref=dst,
             send_sem=self.send_sem.at[index],
-            recv_sem=self.recv_sem.at[index],
+            recv_sem=self.recv_sem.at[index if landing is None else landing],
             device_id=peer,
             device_id_type=MESH,
         )
-        self.started.append(copy)
+        self.started.append((copy, when))
         return copy
 
-    def send(self, src, dst, peer):
-        copy = self.make(src, dst, peer)
-        copy.start()
+    def send(self, src, dst, peer, when=None, landing=None):
+        copy = self.make(src, dst, peer, when, landing)
+        if when is None:
+            copy.start()
+        else:
+            pl.when(when)(copy.start)
         return copy
 
 
-class Ring:
-    def __init__(self, links, full, depth, low, size, relief, rows=()):
+class Spread:
+    def __init__(self, links, full, depth, low, size, relief, relay, rows=()):
         self.links, self.full, self.depth, self.low, self.size = links, full, depth, low, size
         self.relief = relief and links.nz > 1
+        self.relay = relay and links.nz > 2
         self.rows = rows
         self.z_copy, self.y_copy, self.core_copy, self.row_copy = {}, {}, {}, {}
+        self.z_index, self.y_index = {}, {}
+        for t in range(links.nz):
+            when = None
+            if self.relief and t in (1, links.nz - 1):
+                when = links.z % 2 == (0 if t == 1 else 1)
+            block = self.block(links.z - t, links.y)
+            self.y_index[t] = len(links.started)
+            self.y_copy[t] = links.make(block, block, links.y_peer, when)
 
     def place(self, z, y):
         owner = self.links.at(z, y, self.links.core)
@@ -104,13 +122,26 @@
                     self.core_copy[kind, t, r] = links.send(block, block, links.core_peer)
 
     def begin_z(self):
-        own = self.block(self.links.z, self.links.y)
-        self.z_copy[0] = self.links.send(own, own, self.links.z_next)
+        links = self.links
+        nz = links.nz
+        own = self.block(links.z, links.y)
+        for t in map(links.turn, sorted(range(1, nz), key=lambda t: -min(t, nz - t))):
+            when = None
+            if self.relay:
+                when = {1: links.z != nz - 1, nz - 1: links.z != 0}.get(t)
+            self.z_index[t] = len(links.started)
+            self.z_copy[t] = links.send(own, own, links.along(t), when)
         self.to_core(("z", 0), own)
 
+    def to_y(self, t):
+        when = self.links.started[self.y_index[t]][1]
+        if when is None:
+            self.y_copy[t].start()
+        else:
+            pl.when(when)(self.y_copy[t].start)
+
     def begin_y(self):
-        own = self.block(self.links.z, self.links.y)
-        self.y_copy[0] = self.links.send(own, own, self.links.y_peer)
+        self.to_y(0)
 
     def begin(self):
         self.begin_z()
@@ -118,26 +149,34 @@
 
     def along(self, t):
         links = self.links
-        self.z_copy[t - 1].wait_recv()
+        t = links.turn(t)
+        nz = links.nz
+        self.z_copy[t].wait_recv()
         block = self.block(links.z - t, links.y)
-        if t < links.nz - 1:
-            self.z_copy[t] = links.send(block, block, links.z_next)
-        if not (self.relief and t == 1):
-            self.y_copy[t] = links.send(block, block, links.y_peer)
+        if self.relay and t == 2:
+            links.send(block, block, links.along(nz - 1), links.z == 1, self.z_index[1])
+        if self.relay and t == nz - 2:
+            links.send(block, block, links.along(1), links.z == nz - 2, self.z_index[nz - 1])
+        self.to_y(t)
         self.to_core(("z", t), block)
 
     def across(self, t):
+        t = self.links.turn(t)
+        self.y_copy[t].wait_recv()
+        self.to_core(("y", t), self.block(self.links.z - t, 1 - self.links.y))
+
+    def pass_on(self):
         links = self.links
-        block = self.block(links.z - t, 1 - links.y)
-        if self.relief and t == 1:
-            self.extra.wait_recv()
-        else:
-            self.y_copy[t].wait_recv()
-            if self.relief and t == 0:
-                self.extra = links.send(block, block, links.z_next)
-        self.to_core(("y", t), block)
+        self.across(0)
+        if self.relief:
+            block = self.block(links.z, 1 - links.y)
+            even = links.z % 2 == 0
+            partner = (links.row, links.at(links.z + 1 - 2 * (links.z % 2), links.y, links.core))
+            landing = jnp.where(even, self.y_index[1], self.y_index[links.nz - 1])
+            links.send(block, block, partner, None, landing)
 
     def arrive(self, t):
+        t = self.links.turn(t)
         self.core_copy["z", t].wait_recv()
         self.core_copy["y", t].wait_recv()
 
@@ -148,14 +187,15 @@
 
 def layer_kernel(n_row, n_col, dims, side, *refs):
     local_rows, cols, depth, width, hidden = dims
-    shifts, tok_in, q_in, o_in, u_in, d_in, gain, attn_rate, mlp_rate, hidden_gain, out = refs[:11]
+    shifts, tok_in, q_in, o_in, u_in, d_in = refs[:6]
+    vectors, out = refs[6:10], refs[10]
     q_full, o_all, u_full, d_full, tok, piece, sphere_all = refs[11:18]
     strip, q_all, kv_all, back, home_all = refs[18:23]
     mixed_all, active, down_send, down_recv, down_own = refs[23:28]
     local_sem, send_sem, recv_sem, kv_send, kv_recv, back_send, back_recv = refs[28:35]
-    home_send, home_recv = refs[35:]
-
-    links = Links(n_row, n_col, send_sem, recv_sem)
+    home_send, home_recv, gain, attn_rate, mlp_rate, hidden_gain = refs[35:]
+
+    links = Links(n_row, n_col, side, send_sem, recv_sem)
     row, col, nz = links.row, links.col, links.nz
     own = local_rows * cols
     rows = local_rows * n_row
@@ -182,6 +222,7 @@
                 (u_in, u_full.at[here]),
                 (d_in, d_full.at[here]),
             ]
+            + list(zip(vectors, (gain, attn_rate, mlp_rate, hidden_gain)))
         )
     ]
     for copy in local:
@@ -190,27 +231,27 @@
     links.greet([mate(k) for k in range(1, per_window)])
 
     half = share // 2
-    q_a, q_b = [Ring(links, q_full, share, k * half, half, k == 0) for k in range(2)]
+    q_a = Spread(links, q_full, share, 0, half, True, False)
+    q_b = Spread(links, q_full, share, half, half, False, True)
     o_rows = [(r, o_all.at[r]) for r in range(1, n_row)]
-    o_a = Ring(links, o_all.at[0], share, 0, share, False, o_rows)
-    u_a, u_b = [Ring(links, u_full, share, k * half, half, k == 0) for k in range(2)]
-    d_a, d_b = [Ring(links, d_full, share, k * half, half, k == 0) for k in range(2)]
+    o_a = Spread(links, o_all.at[0], share, 0, share, False, True, o_rows)
+    u_a = Spread(links, u_full, share, 0, half, True, True)
+    u_b = Spread(links, u_full, share, half, half, False, True)
+    d_a = Spread(links, d_full, share, 0, half, False, True)
+    d_b = Spread(links, d_full, share, half, half, True, True)
 
     chunk = band
     steps = own // chunk
-    local[3].wait()
-    halo = []
-    for i in range(steps):
-        part = slice(i * chunk, (i + 1) * chunk)
-        value = to_sphere(tok[part, :].astype(F32)).astype(BF)
-        sphere_all[0, part, :] = value
-        piece[mine, part, :] = value
-        halo.append(links.send(piece.at[mine, part], piece.at[1 - mine, part], target))
-    for copy in local[:3]:
-        copy.wait()
-    q_a.begin()
-    q_b.begin()
-
+    half_steps = steps // 2
+    early, late = range(half_steps), range(half_steps, steps)
+    halo = [
+        links.make(
+            piece.at[mine, pl.ds(i * chunk, chunk)],
+            piece.at[1 - mine, pl.ds(i * chunk, chunk)],
+            target,
+        )
+        for i in range(steps)
+    ]
     bits = cols.bit_length() - 1
 
     def one_hot(length, row_step, column_step, per_piece):
@@ -240,53 +281,22 @@
         for i in range(steps)
     ]
 
-    def shift_columns():
-        for i in range(steps):
-            part = slice(i * chunk, (i + 1) * chunk)
-            halo[i].wait_recv()
-            near = jnp.concatenate([piece[k, part, :] for k in range(2)], axis=0)
-            strip[0, part, :] = jnp.dot(to_columns, near, preferred_element_type=F32).astype(BF)
-            for copy in spread[i]:
-                copy.start()
-
     inside = links.core == (0 if side > 0 else 1)
-    pl.when(inside)(shift_columns)
-    for ring in (q_a, q_b):
-        ring.across(0)
-        ring.along(1)
-    pl.when(jnp.logical_not(inside))(shift_columns)
-    local[4].wait()
-    o_a.begin()
-    q_a.along(2)
-    q_a.across(1)
-    q_b.along(2)
-    q_b.across(1)
-    local[5].wait()
-    u_a.begin_z()
-    for ring in (q_a, q_b):
-        for t in range(3, nz):
-            ring.along(t)
-        ring.across(2)
-    u_a.begin_y()
-    u_b.begin_z()
-    around = [
-        links.send(sphere_all.at[0], sphere_all.at[r], links.other_row(r))
-        for r in range(1, n_row)
-    ]
-    o_a.along(1)
-    o_a.across(0)
-    for ring in (q_a, q_b):
-        for t in range(3, nz):
-            ring.across(t)
-    u_b.begin_y()
-    o_a.along(2)
-    o_a.across(1)
-    u_a.along(1)
-    for sent in spread:
-        for copy in sent:
-            copy.wait_recv()
-    q_a.arrive_all()
-    q_b.arrive_all()
+    outside = jnp.logical_not(inside)
+
+    def shift_columns(who, which):
+        @pl.when(who)
+        def _():
+            for i in which:
+                part = slice(i * chunk, (i + 1) * chunk)
+                halo[i].wait_recv()
+                near = jnp.concatenate([piece[k, part, :] for k in range(2)], axis=0)
+                strip[0, part, :] = jnp.dot(
+                    to_columns, near, preferred_element_type=F32
+                ).astype(BF)
+                for copy in spread[i]:
+                    copy.start()
+
     group = (lax.broadcasted_iota(jnp.int32, (LANES, LANES), 0) < HD) == (
         lax.broadcasted_iota(jnp.int32, (LANES, LANES), 1) < HD
     )
@@ -383,20 +393,6 @@
         attend(b - 1, 0)
         return carry
 
-    project(0, 0)
-    u_b.along(1)
-    u_a.across(0)
-    u_b.across(0)
-    lax.fori_loop(1, bands, project_attend, 0)
-    attend(bands - 1, 0)
-    u_a.along(2)
-    u_b.along(2)
-    for t in range(3, nz):
-        o_a.along(t)
-    o_a.across(2)
-    local[6].wait()
-    d_a.begin_z()
-
     def go_home(j, carry):
         b = lax.rem(j + 1, bands)
 
@@ -418,23 +414,6 @@
         for r in range(1, n_row):
             home_copy(b, r).start()
         return carry
-
-    lax.fori_loop(0, bands, go_home, 0)
-    u_a.across(1)
-    u_b.across(1)
-    d_b.begin_z()
-    for t in range(3, nz):
-        o_a.across(t)
-    d_a.begin_y()
-    d_b.begin_y()
-    for ring in (u_a, u_b):
-        for t in range(3, nz):
-            ring.along(t)
-        ring.across(2)
-    o_a.beyond()
-    o_a.arrive_all()
-    for copy in around:
-        copy.wait_recv()
 
     def mix(j, carry):
         b = lax.rem(j + 1, bands)
@@ -453,16 +432,6 @@
         mixed_all[slot, part, :] = value.astype(BF)
         return carry
 
-    lax.fori_loop(0, bands, mix, 0)
-    d_a.along(1)
-    d_b.along(1)
-    d_a.across(0)
-    d_b.across(0)
-    for ring in (u_a, u_b):
-        for t in range(3, nz):
-            ring.across(t)
-    u_a.arrive_all()
-    u_b.arrive_all()
     tile = min(512, hidden)
 
     def raise_slot(r):
@@ -477,36 +446,164 @@
 
         lax.fori_loop(0, hidden // tile, raise_tile, 0)
 
-    raise_slot(0)
-    for ring in (d_a, d_b):
-        ring.along(2)
-        ring.across(1)
+    span = 4 * share
+    lowered = []
+
+    def lower_to(r, t):
+        z = lax.rem(links.z - links.turn(t) + nz, nz)
+        weight = d_full[pl.ds(pl.multiple_of(z * span, span), span), :]
+        return z, lax.dot_general(active[r], weight, LAST, preferred_element_type=F32)
+
+    def lower(t):
+        d_a.arrive(t)
+        d_b.arrive(t)
+        for r in range(1, n_row):
+            z, got = lower_to(r, t)
+            down_send[r, z] = got.astype(BF)
+            lowered.append(
+                links.send(
+                    down_send.at[r, z], down_recv.at[r, z], links.other_row(n_row - r)
+                )
+            )
+
+    def lower_own(t):
+        z, got = lower_to(0, t)
+        down_own[z] = got
+
+    def to_neighbour():
+        for i in range(steps):
+            part = slice(i * chunk, (i + 1) * chunk)
+            value = to_sphere(tok[part, :].astype(F32)).astype(BF)
+            sphere_all[0, part, :] = value
+            piece[mine, part, :] = value
+
+    for copy in local[:3]:
+        copy.wait()
+    q_b.begin_z()
+    q_b.begin_y()
+    local[5].wait()
+    u_b.begin_y()
+    local[4].wait()
+    o_a.begin_y()
+    local[3].wait()
+    to_neighbour()
+    for i in early:
+        halo[i].start()
+    around = [
+        links.send(sphere_all.at[0], sphere_all.at[r], links.other_row(r))
+        for r in range(1, n_row)
+    ]
+    shift_columns(inside, early)
+    q_a.begin_z()
+    q_a.begin_y()
+    for i in late:
+        halo[i].start()
+    q_b.along(2)
+    for copy in around:
+        copy.wait_recv()
+    o_a.begin_z()
+    q_b.along(1)
+    u_a.begin_y()
+    shift_columns(outside, early)
+    u_b.pass_on()
+    q_b.pass_on()
+    q_b.across(2)
+    shift_columns(inside, late)
+    q_a.pass_on()
+    q_a.along(2)
+    q_a.along(1)
+    for t in range(3, nz):
+        q_b.along(t)
+    for t in range(3, nz):
+        q_a.along(t)
+    o_a.along(2)
+    o_a.along(1)
+    o_a.pass_on()
+    u_b.begin_z()
+    for t in range(3, nz):
+        o_a.along(t)
+    q_a.across(2)
+    q_a.across(1)
+    u_b.along(2)
+    shift_columns(outside, late)
+    u_a.begin_z()
+    o_a.across(2)
+    local[6].wait()
+    d_a.begin_y()
+    for t in range(3, nz):
+        q_b.across(t)
+    d_b.begin_y()
+    u_b.along(1)
+    q_b.across(1)
+    for t in range(3, nz):
+        o_a.across(t)
+    for sent in spread:
+        for copy in sent:
+            copy.wait_recv()
+    for t in range(3, nz):
+        q_a.across(t)
+    for t in range(3, nz):
+        u_b.along(t)
+    u_a.along(2)
+    d_a.begin_z()
+    for copy in local[7:]:
+        copy.wait()
+    q_a.arrive_all()
+    q_b.arrive_all()
+    o_a.across(1)
+    project(0, 0)
+    lax.fori_loop(1, bands, project_attend, 0)
+    attend(bands - 1, 0)
+    u_a.pass_on()
+    for t in range(3, nz):
+        u_b.across(t)
+    for t in range(3, nz):
+        u_a.along(t)
+    o_a.beyond()
+    lax.fori_loop(0, bands, go_home, 0)
+    u_a.along(1)
+    d_b.begin_z()
+    u_a.across(2)
+    u_b.across(2)
+    d_a.along(2)
+    for t in range(3, nz):
+        u_a.across(t)
+    d_b.along(2)
+    u_a.across(1)
+    o_a.arrive_all()
+    d_a.pass_on()
+    d_b.pass_on()
+    u_b.across(1)
+    lax.fori_loop(0, bands, mix, 0)
+    d_a.along(1)
+    d_a.across(2)
+    d_b.across(2)
+    u_a.arrive_all()
+    u_b.arrive_all()
+    d_b.along(1)
     for r in range(1, n_row):
         raise_slot(r)
-    for ring in (d_a, d_b):
-        for t in range(3, nz):
-            ring.along(t)
-        ring.across(2)
-
-    span = 4 * share
-    lowered = {}
-    for t in range(nz):
-        for ring in (d_a, d_b):
-            if t > 2:
-                ring.across(t)
-            ring.arrive(t)
-        z = lax.rem(links.z - t + nz, nz)
-        weight = d_full[pl.ds(pl.multiple_of(z * span, span), span), :]
-        for r in list(range(1, n_row)) + [0]:
-            got = lax.dot_general(active[r], weight, LAST, preferred_element_type=F32)
-            if r == 0:
-                down_own[z] = got
-            else:
-                down_send[r, z] = got.astype(BF)
-                lowered[t, r] = links.send(
-                    down_send.at[r, z], down_recv.at[r, z], links.other_row(n_row - r)
-                )
-    for copy in lowered.values():
+    for t in range(3, nz):
+        d_a.along(t)
+    lower(0)
+    lower(2)
+    for t in range(3, nz):
+        d_b.along(t)
+    d_b.across(1)
+    d_a.across(1)
+    lower(1)
+    for t in range(3, nz):
+        d_a.across(t)
+    for t in range(3, nz):
+        d_b.across(t)
+    for t in range(3, nz):
+        lower(t)
+    raise_slot(0)
+    lower_own(0)
+    lower_own(2)
+    for t in [1] + list(range(3, nz)):
+        lower_own(t)
+    for copy in lowered:
         copy.wait_recv()
     for i in range(steps):
         part = slice(i * chunk, (i + 1) * chunk)
@@ -519,9 +616,11 @@
         base = mixed_all[0, part, :].astype(F32)
         total = to_sphere(jnp.concatenate(pieces, axis=1))
         out[part, :] = to_sphere(base + mlp_rate[...] * (total - base)).astype(BF)
-
-    for copy in links.started:
-        copy.wait_send()
+    for copy, when in links.started:
+        if when is None:
+            copy.wait_send()
+        else:
+            pl.when(when)(copy.wait_send)
 
     def drain(b, carry):
         for k in range(1, per_window):
@@ -560,7 +659,7 @@
     nz = n_col // 4
     span = 4 * share
     steps = own // (WIN * cols)
-    copies = 7 * 4 * nz + steps * n_row + (n_row - 1) * (5 * nz + 1)
+    copies = 7 * (4 * nz + 2) + steps * n_row + (n_row - 1) * (5 * nz + 1)
     dma = pltpu.SemaphoreType.DMA
     dims = (local_rows, cols, depth, width, hidden)
 
@@ -568,7 +667,7 @@
         return pl.pallas_call(
         functools.partial(layer_kernel, n_row, n_col, dims, side),
         out_shape=jax.ShapeDtypeStruct((own, depth), BF),
-        in_specs=[SMEM] + [ANY] * 5 + [VMEM] * 4,
+        in_specs=[SMEM] + [ANY] * 9,
         out_specs=VMEM,
         scratch_shapes=[
             pltpu.VMEM((depth, 3 * width), BF),
@@ -588,7 +687,7 @@
             pltpu.VMEM((n_row, nz, own, span), BF),
             pltpu.VMEM((n_row, nz, own, span), BF),
             pltpu.VMEM((nz, own, span), F32),
-            dma((7,)),
+            dma((11,)),
             dma((copies,)),
             dma((copies,)),
             dma((bands, per_window)),
@@ -597,6 +696,10 @@
             dma((bands,)),
             dma((bands, n_row)),
             dma((bands, n_row)),
+            pltpu.VMEM((1, width), F32),
+            pltpu.VMEM((1, depth), F32),
+            pltpu.VMEM((1, depth), F32),
+            pltpu.VMEM((1, hidden), F32),
         ],
         compiler_params=pltpu.CompilerParams(
             collective_id=0 if side > 0 else 1, has_side_effects=True, vmem_limit_bytes=62 * 1024 * 1024

time: 110 us -> 96.7 us (0.88); the launches traced: 109 us -> 96.8 us
  Pallas kernels: 104 us -> 92.5 us
    pallas_call x1, Pallas kernels: 104 us -> 92.5 us  [layer(): pl.pallas_call(functools.partial(layer_kernel, n_row, n_col, dims, side),...]
where the time goes in v3:
time: 96.7 us; the launch traced here: 96.8 us
  Pallas kernels  92.5 us (96%)
  local copies, waits for them, and re-layouts  3.41 us (4%)
    pallas_call x1, Pallas kernels, layer(): pl.pallas_call(functools.partial(layer_kernel, n_row, n_col, dims, side),...  92.5 us

profile of v3, /device:TPU:0, one launch (start us, length us, event | category | flops | bytes accessed | tf_op | source)
XLA Modules:
  0.0 96.8 jit_solution(18261070403368483553)
XLA Ops:
  0.0 0.0 copy-start
  0.0 1.2 %slice.3 = s32[1]{0:T(128)} slice(s32[2]{0:T(128)} %param.13), slice={[1:2]} | slice | bytes 8 | tf_op jit(solution)/shard_map/slice | solution.py:711
  1.9 0.0 copy-start.1
  1.9 0.0 copy-start.6
  1.9 0.0 copy-done
  1.9 0.7 copy-done.1
  2.6 0.0 copy-done.6
  2.6 93.4 %conditional.1 = (bf16[32,8,1024]{2,1,0:T(8,128)(2,1)S(1)}) conditional(s32[]{:T(128)} %bitcast.12, (s32[2]{0:T(128)S(1)}, bf16[32,8,1024]{2,1,0:T(8,128)(2,1)}, bf16[3,64,512]{2,1,0:T(8,128)(2,1)}, bf16[64,512]{1,0:T(8,128)(2,1)}, bf16[64,2048]{1,0:T(8,128)(2,1)}, /*index=5*/bf16[64,2048]{1,0:T(8,128)(2,1)}, f32[512]{0:T(512)}, f32[1024]{0:T(1024)S(1)}, ...), branch_computations={%region_0.0_spmd, %region_1.0_spmd} | conditional | bytes 24640 | solution.py:710
  2.6 0.0 copy-start.3
  2.6 0.0 copy-start.5
  2.6 0.7 copy-done.3
  3.3 0.0 copy-done.5
  3.3 92.5 %layer.3 = bf16[256,1024]{1,0:T(8,128)(2,1)S(1)} custom-call(s32[2]{0:T(128)S(1)} %get-tuple-element.59.refs_0_, bf16[256,1024]{1,0:T(8,128)(2,1)} %bitcast.17, bf16[3,64,512]{2,1,0:T(8,128)(2,1)} %get-tuple-element.61.refs_2_, bf16[64,512]{1,0:T(8,128)(2,1)} %get-tuple-element.62.refs_3_, bf16[64,2048]{1,0:T(8,128)(2,1)} %get-tuple-element.85.refs_4_, ...), custom_call_target="tpu_custom_call" | custom-call | tf_op jit(solution)/shard_map/cond/branch_1_fun/layer/pallas_call | solution.py:667
  96.0 0.8 copy.28
Async XLA Ops:
  0.0 1.9 %copy-start = (f32[2048]{0:T(1024)S(1)}, f32[2048]{0:T(1024)}, u32[]{:S(2)}) copy-start(f32[2048]{0:T(1024)} %param.21) | copy-start | bytes 24580
  1.9 0.7 copy-start.1
  1.9 0.7 copy-start.6
  2.6 0.7 copy-start.3
  2.6 0.7 copy-start.5

commit v4 on v3

--- a/solution.py
+++ b/solution.py
@@ -16,7 +16,7 @@
 F32 = jnp.float32
 MESH = pl.DeviceIdType.MESH
 VMEM = pl.BlockSpec(memory_space=pltpu.VMEM)
-ANY = pl.BlockSpec(memory_space=pl.ANY)
+HBM = pl.BlockSpec(memory_space=pltpu.HBM)
 SMEM = pl.BlockSpec(memory_space=pltpu.SMEM)
 LAST = (((1,), (1,)), ((), ()))
 
@@ -662,12 +662,13 @@
     copies = 7 * (4 * nz + 2) + steps * n_row + (n_row - 1) * (5 * nz + 1)
     dma = pltpu.SemaphoreType.DMA
     dims = (local_rows, cols, depth, width, hidden)
+    room = 67043328 - own * depth * 2 - 2048
 
     def layer(side, *operands):
         return pl.pallas_call(
         functools.partial(layer_kernel, n_row, n_col, dims, side),
         out_shape=jax.ShapeDtypeStruct((own, depth), BF),
-        in_specs=[SMEM] + [ANY] * 9,
+        in_specs=[SMEM] + [HBM] * 9,
         out_specs=VMEM,
         scratch_shapes=[
             pltpu.VMEM((depth, 3 * width), BF),
@@ -702,7 +703,7 @@
             pltpu.VMEM((1, hidden), F32),
         ],
         compiler_params=pltpu.CompilerParams(
-            collective_id=0 if side > 0 else 1, has_side_effects=True, vmem_limit_bytes=62 * 1024 * 1024
+            collective_id=0 if side > 0 else 1, has_side_effects=True, vmem_limit_bytes=room
         ),
         name="layer",
     )(*operands)

time: 96.7 us -> 95.7 us (0.990)
  local copies, waits for them, and re-layouts: 3.41 us -> 2.03 us
where the time goes in v4:
time: 95.7 us; the launch traced here: 95.5 us
  Pallas kernels  92.6 us (97%)
  local copies, waits for them, and re-layouts  2.03 us (2%)
    pallas_call x1, Pallas kernels, layer(): pl.pallas_call(functools.partial(layer_kernel, n_row, n_col, dims, side),...  92.6 us

profile of v4, /device:TPU:0, one launch (start us, length us, event | category | flops | bytes accessed | tf_op | source)
XLA Modules:
  0.0 95.5 jit_solution(17852262162936190001)
XLA Ops:
  0.0 1.2 %slice.3 = s32[1]{0:T(128)} slice(s32[2]{0:T(128)} %param.13), slice={[1:2]} | slice | bytes 8 | tf_op jit(solution)/shard_map/slice | solution.py:712
  1.9 92.9 %conditional.1 = (bf16[32,8,1024]{2,1,0:T(8,128)(2,1)S(1)}) conditional(s32[]{:T(128)} %bitcast.12, (s32[2]{0:T(128)}, bf16[32,8,1024]{2,1,0:T(8,128)(2,1)}, bf16[3,64,512]{2,1,0:T(8,128)(2,1)}, bf16[64,512]{1,0:T(8,128)(2,1)}, bf16[64,2048]{1,0:T(8,128)(2,1)}, /*index=5*/bf16[64,2048]{1,0:T(8,128)(2,1)}, f32[512]{0:T(512)}, f32[1024]{0:T(1024)}, ...), branch_computations={%region_0.0_spmd, %region_1.0_spmd} | conditional | bytes 8 | solution.py:711
  1.9 92.6 %layer.3 = bf16[256,1024]{1,0:T(8,128)(2,1)S(1)} custom-call(s32[2]{0:T(128)} %get-tuple-element.59.refs_0_, bf16[256,1024]{1,0:T(8,128)(2,1)} %bitcast.17, bf16[3,64,512]{2,1,0:T(8,128)(2,1)} %get-tuple-element.61.refs_2_, bf16[64,512]{1,0:T(8,128)(2,1)} %get-tuple-element.62.refs_3_, bf16[64,2048]{1,0:T(8,128)(2,1)} %get-tuple-element.85.refs_4_, ...), custom_call_target="tpu_custom_call" | custom-call | tf_op jit(solution)/shard_map/cond/branch_1_fun/layer/pallas_call | solution.py:668
  94.8 0.8 copy.28

commit v5 on v4

--- a/solution.py
+++ b/solution.py
@@ -231,13 +231,13 @@
     links.greet([mate(k) for k in range(1, per_window)])
 
     half = share // 2
-    q_a = Spread(links, q_full, share, 0, half, True, False)
+    q_a = Spread(links, q_full, share, 0, half, False, True)
     q_b = Spread(links, q_full, share, half, half, False, True)
     o_rows = [(r, o_all.at[r]) for r in range(1, n_row)]
     o_a = Spread(links, o_all.at[0], share, 0, share, False, True, o_rows)
     u_a = Spread(links, u_full, share, 0, half, True, True)
     u_b = Spread(links, u_full, share, half, half, False, True)
-    d_a = Spread(links, d_full, share, 0, half, False, True)
+    d_a = Spread(links, d_full, share, 0, half, True, True)
     d_b = Spread(links, d_full, share, half, half, True, True)
 
     chunk = band
@@ -479,123 +479,123 @@
 
     for copy in local[:3]:
         copy.wait()
-    q_b.begin_z()
-    q_b.begin_y()
-    local[5].wait()
-    u_b.begin_y()
     local[4].wait()
-    o_a.begin_y()
+    o_a.begin_z()
+    local[6].wait()
+    d_a.begin_y()
+    q_a.begin_z()
+    q_a.begin_y()
     local[3].wait()
     to_neighbour()
     for i in early:
         halo[i].start()
+    q_b.begin_y()
+    o_a.begin_y()
+    local[5].wait()
+    u_b.begin_y()
     around = [
         links.send(sphere_all.at[0], sphere_all.at[r], links.other_row(r))
         for r in range(1, n_row)
     ]
     shift_columns(inside, early)
-    q_a.begin_z()
-    q_a.begin_y()
+    q_a.along(2)
+    q_b.begin_z()
+    q_a.pass_on()
+    o_a.along(2)
+    q_a.along(1)
+    o_a.along(1)
+    u_a.begin_y()
+    for t in range(3, nz):
+        o_a.along(t)
+    q_a.across(2)
     for i in late:
         halo[i].start()
+    u_b.begin_z()
+    o_a.pass_on()
+    shift_columns(inside, late)
+    o_a.across(2)
+    o_a.across(1)
+    q_a.across(1)
     q_b.along(2)
-    for copy in around:
-        copy.wait_recv()
-    o_a.begin_z()
     q_b.along(1)
-    u_a.begin_y()
+    for t in range(3, nz):
+        q_a.along(t)
     shift_columns(outside, early)
-    u_b.pass_on()
+    for t in range(3, nz):
+        q_b.along(t)
+    u_b.along(2)
     q_b.pass_on()
-    q_b.across(2)
-    shift_columns(inside, late)
-    q_a.pass_on()
-    q_a.along(2)
-    q_a.along(1)
-    for t in range(3, nz):
-        q_b.along(t)
-    for t in range(3, nz):
-        q_a.along(t)
-    o_a.along(2)
-    o_a.along(1)
-    o_a.pass_on()
-    u_b.begin_z()
-    for t in range(3, nz):
-        o_a.along(t)
-    q_a.across(2)
-    q_a.across(1)
-    u_b.along(2)
     shift_columns(outside, late)
     u_a.begin_z()
-    o_a.across(2)
-    local[6].wait()
-    d_a.begin_y()
-    for t in range(3, nz):
-        q_b.across(t)
     d_b.begin_y()
     u_b.along(1)
     q_b.across(1)
-    for t in range(3, nz):
-        o_a.across(t)
+    u_a.along(2)
+    q_b.across(2)
+    for t in range(3, nz):
+        q_a.across(t)
+    for t in range(3, nz):
+        u_b.along(t)
+    u_a.pass_on()
+    d_a.begin_z()
+    for t in range(3, nz):
+        q_b.across(t)
     for sent in spread:
         for copy in sent:
             copy.wait_recv()
-    for t in range(3, nz):
-        q_a.across(t)
-    for t in range(3, nz):
-        u_b.along(t)
-    u_a.along(2)
-    d_a.begin_z()
     for copy in local[7:]:
         copy.wait()
     q_a.arrive_all()
     q_b.arrive_all()
-    o_a.across(1)
+    for t in range(3, nz):
+        o_a.across(t)
     project(0, 0)
     lax.fori_loop(1, bands, project_attend, 0)
     attend(bands - 1, 0)
-    u_a.pass_on()
+    u_b.pass_on()
+    o_a.beyond()
+    u_b.across(2)
+    for t in range(3, nz):
+        u_a.along(t)
+    u_a.along(1)
+    u_b.across(1)
+    d_b.begin_z()
+    for copy in around:
+        copy.wait_recv()
+    lax.fori_loop(0, bands, go_home, 0)
+    u_a.across(1)
+    d_b.along(2)
+    u_a.across(2)
+    o_a.arrive_all()
     for t in range(3, nz):
         u_b.across(t)
     for t in range(3, nz):
-        u_a.along(t)
-    o_a.beyond()
-    lax.fori_loop(0, bands, go_home, 0)
-    u_a.along(1)
-    d_b.begin_z()
-    u_a.across(2)
-    u_b.across(2)
+        u_a.across(t)
     d_a.along(2)
-    for t in range(3, nz):
-        u_a.across(t)
-    d_b.along(2)
-    u_a.across(1)
-    o_a.arrive_all()
+    d_b.pass_on()
     d_a.pass_on()
-    d_b.pass_on()
-    u_b.across(1)
     lax.fori_loop(0, bands, mix, 0)
-    d_a.along(1)
-    d_a.across(2)
+    d_b.along(1)
     d_b.across(2)
+    for t in range(3, nz):
+        d_b.along(t)
     u_a.arrive_all()
     u_b.arrive_all()
-    d_b.along(1)
     for r in range(1, n_row):
         raise_slot(r)
+    d_a.along(1)
+    lower(0)
     for t in range(3, nz):
         d_a.along(t)
-    lower(0)
+    d_a.across(2)
     lower(2)
-    for t in range(3, nz):
-        d_b.along(t)
     d_b.across(1)
     d_a.across(1)
+    for t in range(3, nz):
+        d_a.across(t)
+    for t in range(3, nz):
+        d_b.across(t)
     lower(1)
-    for t in range(3, nz):
-        d_a.across(t)
-    for t in range(3, nz):
-        d_b.across(t)
     for t in range(3, nz):
         lower(t)
     raise_slot(0)

time: 95.7 us -> 95 us (level)
  no operation moved by 1% of the time
where the time goes in v5:
time: 95 us; the launch traced here: 95.4 us
  Pallas kernels  92.5 us (97%)
  local copies, waits for them, and re-layouts  2.03 us (2%)
    pallas_call x1, Pallas kernels, layer(): pl.pallas_call(functools.partial(layer_kernel, n_row, n_col, dims, side),...  92.5 us

profile of v5, /device:TPU:0, one launch (start us, length us, event | category | flops | bytes accessed | tf_op | source)
XLA Modules:
  0.0 95.4 jit_solution(6034714671874391965)
XLA Ops:
  0.0 1.2 %slice.3 = s32[1]{0:T(128)} slice(s32[2]{0:T(128)} %param.13), slice={[1:2]} | slice | bytes 8 | tf_op jit(solution)/shard_map/slice | solution.py:712
  1.9 92.7 %conditional.1 = (bf16[32,8,1024]{2,1,0:T(8,128)(2,1)S(1)}) conditional(s32[]{:T(128)} %bitcast.12, (s32[2]{0:T(128)}, bf16[32,8,1024]{2,1,0:T(8,128)(2,1)}, bf16[3,64,512]{2,1,0:T(8,128)(2,1)}, bf16[64,512]{1,0:T(8,128)(2,1)}, bf16[64,2048]{1,0:T(8,128)(2,1)}, /*index=5*/bf16[64,2048]{1,0:T(8,128)(2,1)}, f32[512]{0:T(512)}, f32[1024]{0:T(1024)}, ...), branch_computations={%region_0.0_spmd, %region_1.0_spmd} | conditional | bytes 8 | solution.py:711
  1.9 92.5 %layer.3 = bf16[256,1024]{1,0:T(8,128)(2,1)S(1)} custom-call(s32[2]{0:T(128)} %get-tuple-element.59.refs_0_, bf16[256,1024]{1,0:T(8,128)(2,1)} %bitcast.17, bf16[3,64,512]{2,1,0:T(8,128)(2,1)} %get-tuple-element.61.refs_2_, bf16[64,512]{1,0:T(8,128)(2,1)} %get-tuple-element.62.refs_3_, bf16[64,2048]{1,0:T(8,128)(2,1)} %get-tuple-element.85.refs_4_, ...), custom_call_target="tpu_custom_call" | custom-call | tf_op jit(solution)/shard_map/cond/branch_1_fun/layer/pallas_call | solution.py:668
  94.6 0.8 copy.28
